TPU v7x, 32 devices: a whole 2x2x4 slice. The times are simulated.
32 devices in a mesh: band: 16 (over z, y, x), chan: 2 (over core).
Axes of the slice: x: 2, y: 2, z: 4, core: 2. Of those that a mesh axis runs over, the one named last changes fastest.
Arguments:
- grid_latent: bfloat16 [18432, 512], P(('band', 'chan')), may hold values from -6 to 6
- edge_latent: bfloat16 [36864, 512], P(('band', 'chan')), may hold values from -6 to 6
- mesh_latent: bfloat16 [5120, 512], P(('band', 'chan')), may hold values from -6 to 6
- mesh_cotangent: bfloat16 [5120, 512], P(('band', 'chan')), may hold values from -6 to 6
- w_grid: bfloat16 [512, 512], P(None, 'chan'), may hold values from -0.15625 to 0.15625
- w_mesh: bfloat16 [512, 512], P(None, 'chan'), may hold values from -0.15625 to 0.15625
- w_edge: bfloat16 [512, 512], P(None, 'chan'), may hold values from -0.15625 to 0.15625
- bias: float32 [512], P('chan'), may hold values from -3 to 3
- w_out: bfloat16 [512, 512], P('chan'), may hold values from -0.25 to 0.25
- senders: int32 [36864], P('band'), may hold values from 0 to 18431, as said below
- receivers: int32 [36864], P('band'), may hold values from 0 to 5119, as said below
- edge_count: int32 [16], P('band'), may hold values from 1152 to 2304, as said below
Outputs:
- grad_grid: bfloat16 [18432, 512], P(('band', 'chan'))
- grad_edge: bfloat16 [36864, 512], P(('band', 'chan'))
- grad_mesh: bfloat16 [5120, 512], P(('band', 'chan'))
- grad_w_grid: float32 [512, 512], P(None, 'chan')
- grad_w_mesh: float32 [512, 512], P(None, 'chan')
- grad_w_edge: float32 [512, 512], P(None, 'chan')
- grad_bias: float32 [512], P('chan')
- grad_w_out: float32 [512, 512], P('chan')
Inputs may be any that keep to these rules, and one draw needn't show every extreme that they name: `senders`: an edge of band j (rows j * 2304 to (j + 1) * 2304 - 1) has its sender among grid rows j * 1152 to (j + 1) * 1152 - 1. `receivers`: an edge of band j has its receiver among mesh rows of owners j - 1, j, j + 1 (owner i holds rows i * 320 to (i + 1) * 320 - 1). `edge_count`: some band uses all 2304 slots.
All inputs are finite; a program needn't handle non-finite values.
Results may differ from a plain program's by a relative error of at most 0.0059.
Values may be sent and summed in bfloat16 or wider, within the bound.
A program may use at most 64 MiB of HBM per device.

v0:
```python
import functools

import jax
import jax.numpy as jnp
from jax import lax
from jax.experimental import pallas as pl
from jax.experimental.pallas import tpu as pltpu
from jax.sharding import PartitionSpec as P

BF = jnp.bfloat16
F32 = jnp.float32
MESH = pl.DeviceIdType.MESH
VMEM = pl.BlockSpec(memory_space=pltpu.VMEM)
ANY = pl.BlockSpec(memory_space=pl.ANY)
NN = (((1,), (0,)), ((), ()))
NT = (((1,), (1,)), ((), ()))
TN = (((0,), (0,)), ((), ()))


def mm(a, b, dims=NN):
    return lax.dot_general(a, b, dims, preferred_element_type=F32)


def remote(src, dst, send, recv, device):
    return pltpu.make_async_remote_copy(
        src_ref=src, dst_ref=dst, send_sem=send, recv_sem=recv,
        device_id=device, device_id_type=MESH,
    )


def gather_kernel(n, grid, edge, mesh, cot, grid_oth, edge_oth, win, send, recv, local):
    me, half = lax.axis_index("band"), lax.axis_index("chan")
    up, down = lax.rem(me + 1, n), lax.rem(me + n - 1, n)
    partner = {"band": me, "chan": 1 - half}
    above, below = {"band": up, "chan": half}, {"band": down, "chan": half}
    barrier = pltpu.get_barrier_semaphore()
    for device in (partner, above, below):
        pl.semaphore_signal(barrier, inc=1, device_id=device, device_id_type=MESH)
    pl.semaphore_wait(barrier, 3)
    copies = [
        remote(src, dst, send.at[i], recv.at[i], device)
        for i, (src, dst, device) in enumerate((
            (mesh, win.at[0, 0, 0], above), (cot, win.at[0, 0, 1], above),
            (mesh, win.at[2, 0, 0], below), (cot, win.at[2, 0, 1], below),
            (mesh, win.at[1, 1, 0], partner), (cot, win.at[1, 1, 1], partner),
            (grid, grid_oth, partner), (edge, edge_oth, partner),
        ))
    ]
    own = [
        pltpu.make_async_copy(src, win.at[1, 0, i], local.at[i])
        for i, src in enumerate((mesh, cot))
    ]
    for copy in copies + own:
        copy.start()
    forward = []
    for side in (0, 2):
        copies[side].wait()
        copies[side + 1].wait()
        i = 8 + side // 2
        forward.append(remote(
            win.at[side, 0], win.at[side, 1], send.at[i], recv.at[i], partner))
        forward[-1].start()
    for copy in own + copies[4:] + forward:
        copy.wait()


def turned(x):
    return x.astype(F32).T.astype(BF)


def main_kernel(
    tiles, own_m, used, grid, grid_oth, edge, edge_oth, win, wg, we, wm, wo, bias, sender, receiver,
    grad_edge, grad_grid, rx, gall, gbias,
    wg_t, we_t, bcol, pg, pmc, sg, sr, ge, gb,
):
    t = pl.program_id(0)
    chan, band, count = lax.axis_index("chan"), lax.axis_index("band"), used[0]
    rows, width = grid.shape
    hidden = wg.shape[1]
    window = 3 * own_m
    pad = pmc.shape[1] - window

    def nodes(which):
        rows_in = win[:, :, which].reshape(window, width)
        if pad:
            rows_in = jnp.concatenate([rows_in, jnp.zeros((pad, width), BF)], axis=0)
        return rows_in

    @pl.when(t == 0)
    def _():
        wg_t[...] = turned(wg[...])
        we_t[...] = turned(we[...])
        bcol[...] = jnp.broadcast_to(bias[...], (128, hidden)).T
        pg[:, :rows] = mm(wg_t[...], grid[...], NT).astype(BF)
        pg[:, rows:2 * rows] = mm(wg_t[...], grid_oth[...], NT).astype(BF)
        pmc[:hidden] = mm(nodes(0), wm[...]).T.astype(BF)
        pmc[hidden:] = mm(wo[...], nodes(1), NT).astype(BF)
        sg[...] = jnp.zeros_like(sg)
        sr[...] = jnp.zeros_like(sr)
        ge[...] = jnp.zeros_like(ge)
        gb[...] = jnp.zeros_like(gb)

    tile = edge.shape[0]
    x = jnp.where(t < tiles // 2, edge[...], edge_oth[...])
    place = lax.rem(t + chan * (tiles // 2), tiles)
    from_row = sender[place] - (2 * band + chan) * rows
    from_row = jnp.where(from_row < 0, from_row + 2 * rows, from_row)
    to_row = receiver[place] - (band - 1) * own_m
    owner = jnp.where(to_row >= 2 * own_m, 2 * own_m, jnp.where(to_row >= own_m, own_m, 0))
    inner = to_row - owner - chan * (own_m // 2)
    to_row = owner + jnp.where(inner < 0, inner + own_m, inner)
    slot = lax.broadcasted_iota(jnp.int32, (1, tile), 1) + place * tile
    alive = jnp.where(slot < count, 1.0, 0.0)
    s_t = jnp.where(
        lax.broadcasted_iota(jnp.int32, (2 * rows, tile), 0) == from_row, 1.0, 0.0
    ).astype(BF)
    r_t = jnp.where(
        lax.broadcasted_iota(jnp.int32, (pmc.shape[1], tile), 0) == to_row, 1.0, 0.0
    ).astype(BF)
    both = mm(pmc[...], r_t)
    pre = mm(pg[...], s_t) + both[:hidden] + mm(we_t[...], x, NT) + bcol[:, :1]
    sig = jax.nn.sigmoid(pre)
    act = (pre * sig * alive).astype(BF)
    pre_cot = (both[hidden:] * alive * sig * (1.0 + pre * (1.0 - sig))).astype(BF)
    grad_edge[...] = mm(pre_cot, we_t[...], TN).astype(BF)
    sg[...] += mm(pre_cot, s_t, NT)
    sr[...] += mm(jnp.concatenate([pre_cot, act], axis=0), r_t, NT)
    ge[...] += mm(pre_cot, x)
    rounded = pre_cot.astype(F32)
    total = gb[...]
    for k in range(tile // 128):
        total = total + rounded[:, k * 128:(k + 1) * 128]
    gb[...] = total

    @pl.when(t == tiles - 1)
    def _():
        sums = sg[...].astype(BF)
        grad_grid[...] = mm(sums, wg_t[...], TN).astype(BF)
        parts = gall.shape[1:2] + gall.shape[3:]
        put = lambda v: v.reshape(parts).astype(BF)
        gall[0, :, 0] = put(mm(sums[:, :rows], grid[...]) + mm(sums[:, rows:], grid_oth[...]))
        gall[0, :, 1] = put(ge[...])
        mesh_sums = sr[:hidden]
        gall[1, :, 0] = put(mm(mesh_sums.astype(BF), nodes(0)))
        gall[1, :, 1] = put(mm(sr[hidden:].astype(BF), nodes(1)))
        rx[...] = mesh_sums.T[:window].astype(BF)
        gbias[...] = jnp.broadcast_to(
            jnp.sum(gb[...].T, axis=0, keepdims=True), gbias.shape
        )


def reduce_kernel(
    low, high, grad_edge, grad_grid, rx, gall, gbias, wm,
    edge_in, grid_in, mesh_in, mesh_own, out, bias_out,
    rims, mesh_send, in1, sum1, in2, sum2, out1, bias_in, bias_sum,
    send, recv, s1, r1, s2, r2, s3, r3, s4, r4, sb, rb, sc, rc,
):
    n = low * high
    me, half = lax.axis_index("band"), lax.axis_index("chan")
    mine, plane = lax.rem(me, low), me // low
    up, down = lax.rem(me + 1, n), lax.rem(me + n - 1, n)
    partner = {"band": me, "chan": 1 - half}
    above, below = {"band": up, "chan": half}, {"band": down, "chan": half}

    def low_peer(k):
        return lax.rem(mine + k, low)

    def low_device(k):
        return {"band": plane * low + low_peer(k), "chan": half}

    def high_peer(k):
        return lax.rem(plane + k, high)

    def high_device(k):
        return {"band": high_peer(k) * low + mine, "chan": half}

    barrier = pltpu.get_barrier_semaphore()

    def greet(k, carry):
        pl.semaphore_signal(
            barrier, inc=1, device_id={"band": lax.rem(me + k, n), "chan": half},
            device_id_type=MESH)
        return carry
    pl.semaphore_signal(barrier, inc=1, device_id=partner, device_id_type=MESH)
    lax.fori_loop(1, n, greet, 0)
    pl.semaphore_wait(barrier, n)

    def scatter_low(k, ab):
        return remote(gall.at[ab, low_peer(k)], in1.at[ab, k], s1.at[ab, k], r1.at[ab, k],
                      low_device(k))

    def scatter_high(k, ab):
        return remote(sum1.at[ab, high_peer(k)], in2.at[ab, k], s2.at[ab, k], r2.at[ab, k],
                      high_device(k))

    def gather_high(k, ab):
        return remote(sum2.at[ab], out1.at[ab, plane], s3.at[ab, k], r3.at[ab, k],
                      high_device(k))

    def gather_low(k, ab):
        return remote(out1.at[ab], out.at[ab, mine], s4.at[ab, k], r4.at[ab, k],
                      low_device(k))

    def bias_low(k):
        return remote(gbias, bias_in.at[mine], sb.at[k], rb.at[k], low_device(k))

    def bias_high(k):
        return remote(bias_sum, bias_out.at[plane], sc.at[k], rc.at[k], high_device(k))

    lows, highs = range(1, low), range(1, high)
    for k in lows:
        scatter_low(k, 0).start()
    for k in lows:
        bias_low(k).start()
    raise_up = remote(rx.at[2], rims.at[0], send.at[0], recv.at[0], above)
    lower = remote(rx.at[0], rims.at[1], send.at[1], recv.at[1], below)
    rows_e, rows_g, rows_m = edge_in.shape[0], grid_in.shape[0], mesh_own.shape[0]
    edge_copy = remote(
        grad_edge.at[pl.ds(rows_e, rows_e)], edge_in, send.at[2], recv.at[2], partner)
    grid_copy = remote(
        grad_grid.at[pl.ds(rows_g, rows_g)], grid_in, send.at[3], recv.at[3], partner)
    for k in lows:
        scatter_low(k, 1).start()
    grid_copy.start()
    edge_copy.start()
    raise_up.start()
    lower.start()
    bias_in[mine] = gbias[...]

    def reduce_low(ab):
        for k in lows:
            scatter_low(k, ab).wait()
        total = gall[ab, mine].astype(F32)
        for k in lows:
            total = total + in1[ab, k].astype(F32)
        sum1[ab] = total.astype(BF)
        for k in highs:
            scatter_high(k, ab).start()

    def reduce_high(ab):
        for k in highs:
            scatter_high(k, ab).wait()
        total = sum1[ab, plane].astype(F32)
        for k in highs:
            total = total + in2[ab, k].astype(F32)
        sum2[ab] = total.astype(BF)
        for k in highs:
            gather_high(k, ab).start()
        out1[ab, plane] = sum2[ab]

    def spread(ab):
        for k in highs:
            gather_high(k, ab).wait()
        for k in lows:
            gather_low(k, ab).start()
        out[ab, mine] = out1[ab]

    reduce_low(0)
    for k in lows:
        bias_low(k).wait()
    bias_sum[...] = jnp.sum(bias_in[...], axis=0)
    for k in highs:
        bias_high(k).start()
    bias_out[plane] = bias_sum[...]
    reduce_high(0)
    reduce_low(1)
    spread(0)
    reduce_high(1)
    raise_up.wait()
    lower.wait()
    total = (rx[1].astype(F32) + rims[0].astype(F32) + rims[1].astype(F32)).astype(BF)
    part = mm(total, wm[...], NT)
    mesh_send[...] = part[rows_m:].astype(BF)
    mesh_copy = remote(mesh_send, mesh_in, send.at[4], recv.at[4], partner)
    mesh_copy.start()
    mesh_own[...] = part[:rows_m].astype(BF)
    spread(1)
    grid_copy.wait()
    edge_copy.wait()
    mesh_copy.wait()
    for k in highs:
        bias_high(k).wait()
    for ab in (0, 1):
        for k in lows:
            gather_low(k, ab).wait()


def final_kernel(
    grid_own, grid_in, edge_own, edge_in, mesh_own, mesh_in, out, bias_out,
    grad_grid, grad_edge, grad_mesh, gwg, gwm, gwe, gbias, gwo,
):
    for a, b, to in (
        (grid_own, grid_in, grad_grid), (edge_own, edge_in, grad_edge),
        (mesh_own, mesh_in, grad_mesh),
    ):
        to[...] = (a[...].astype(F32) + b[...].astype(F32)).astype(BF)
    full = lambda ab, i: out[ab, :, i].astype(F32).reshape(gwo.shape)
    gwg[...] = full(0, 0).T
    gwe[...] = full(0, 1).T
    gwm[...] = full(1, 0).T
    gwo[...] = full(1, 1)
    gbias[...] = jnp.sum(bias_out[...], axis=0)[0]


def body(
    grid_latent,
    edge_latent,
    mesh_latent,
    mesh_cotangent,
    w_grid,
    w_mesh,
    w_edge,
    bias,
    w_out,
    senders,
    receivers,
    edge_count,
):
    n = lax.axis_size("band")
    rows_g, width = grid_latent.shape
    rows_e = edge_latent.shape[0]
    rows_m = mesh_latent.shape[0]
    hidden = w_grid.shape[1]
    own_m = 2 * rows_m
    sds = jax.ShapeDtypeStruct
    dma = pltpu.SemaphoreType.DMA
    grid_oth, edge_oth, win = pl.pallas_call(
        functools.partial(gather_kernel, n),
        out_shape=(
            sds(grid_latent.shape, BF), sds(edge_latent.shape, BF),
            sds((3, 2, 2, rows_m, width), BF),
        ),
        in_specs=[ANY, ANY, VMEM, VMEM],
        out_specs=(ANY, ANY, VMEM),
        scratch_shapes=[dma((10,)), dma((10,)), dma((2,))],
        compiler_params=pltpu.CompilerParams(collective_id=0, has_side_effects=True),
    )(grid_latent, edge_latent, mesh_latent, mesh_cotangent)

    tile = rows_e
    tiles = 2 * rows_e // tile
    mid = tiles // 2
    padded = -(-3 * own_m // 128) * 128
    low = 1
    while low * low < n:
        low *= 2
    high = n // low
    rows_c = hidden // n
    whole = lambda *shape: pl.BlockSpec(shape, lambda t: (0,) * len(shape))
    grad_edge, grad_grid, rx, gall, gbias = pl.pallas_call(
        functools.partial(main_kernel, tiles, own_m),
        grid=(tiles,),
        in_specs=[
            pl.BlockSpec(memory_space=pltpu.SMEM),
            whole(rows_g, width), whole(rows_g, width),
            pl.BlockSpec((tile, width), lambda t: (jnp.minimum(t, mid - 1), 0)),
            pl.BlockSpec((tile, width), lambda t: (jnp.maximum(t - mid, 0), 0)),
            whole(3, 2, 2, rows_m, width),
            whole(width, hidden), whole(width, hidden), whole(width, hidden),
            whole(hidden, width), whole(1, hidden),
            whole(tiles, 1, tile), whole(tiles, 1, tile),
        ],
        out_specs=(
            pl.BlockSpec((tile, width), lambda t: (t, 0)),
            whole(2 * rows_g, width), whole(3 * own_m, hidden),
            whole(2, n, 2, rows_c, width), whole(8, hidden),
        ),
        scratch_shapes=[
            pltpu.VMEM((hidden, width), BF), pltpu.VMEM((hidden, width), BF),
            pltpu.VMEM((hidden, 128), F32),
            pltpu.VMEM((hidden, 2 * rows_g), BF), pltpu.VMEM((2 * hidden, padded), BF),
            pltpu.VMEM((hidden, 2 * rows_g), F32), pltpu.VMEM((2 * hidden, padded), F32),
            pltpu.VMEM((hidden, width), F32), pltpu.VMEM((hidden, 128), F32),
        ],
        out_shape=(
            sds((2 * rows_e, width), BF), sds((2 * rows_g, width), BF),
            sds((3 * own_m, hidden), BF),
            sds((2, n, 2, rows_c, width), BF), sds((8, hidden), F32),
        ),
        compiler_params=pltpu.CompilerParams(dimension_semantics=("arbitrary",)),
    )(
        edge_count, grid_latent, grid_oth, edge_latent, edge_oth, win,
        w_grid, w_edge, w_mesh, w_out, bias[None],
        senders.reshape(tiles, 1, tile), receivers.reshape(tiles, 1, tile),
    )

    blocks = (2, rows_c, width)
    edge_in, grid_in, mesh_in, mesh_own, out, bias_out = pl.pallas_call(
        functools.partial(reduce_kernel, low, high),
        out_shape=(
            sds((rows_e, width), BF), sds((rows_g, width), BF),
            sds((rows_m, width), BF), sds((rows_m, width), BF),
            sds((2, low, high) + blocks, BF), sds((high, 8, hidden), F32),
        ),
        in_specs=[ANY, ANY] + [VMEM] * 4,
        out_specs=(ANY, ANY) + (VMEM,) * 4,
        scratch_shapes=[
            pltpu.VMEM((2, own_m, hidden), BF), pltpu.VMEM((rows_m, width), BF),
            pltpu.VMEM((2, low, high) + blocks, BF), pltpu.VMEM((2, high) + blocks, BF),
            pltpu.VMEM((2, high) + blocks, BF), pltpu.VMEM((2,) + blocks, BF),
            pltpu.VMEM((2, high) + blocks, BF),
            pltpu.VMEM((low, 8, hidden), F32), pltpu.VMEM((8, hidden), F32),
            dma((5,)), dma((5,)), dma((2, low)), dma((2, low)), dma((2, high)),
            dma((2, high)), dma((2, high)), dma((2, high)), dma((2, low)), dma((2, low)),
            dma((low,)), dma((low,)), dma((high,)), dma((high,)),
        ],
        compiler_params=pltpu.CompilerParams(collective_id=1, has_side_effects=True),
    )(
        grad_edge, grad_grid, rx.reshape(3, own_m, hidden),
        gall.reshape((2, low, high) + blocks), gbias, w_mesh,
    )

    rows_of = lambda rows: pl.BlockSpec((rows // 2, width), lambda t: (t, 0))
    turned_spec = pl.BlockSpec((width, hidden // 2), lambda t: (0, t))
    grad_grid, grad_edge, grad_mesh, gwg, gwm, gwe, gbias, gwo = pl.pallas_call(
        final_kernel,
        grid=(2,),
        in_specs=[
            rows_of(rows_g), rows_of(rows_g), rows_of(rows_e), rows_of(rows_e),
            rows_of(rows_m), rows_of(rows_m),
            pl.BlockSpec((2, n // 2) + blocks, lambda t: (0, t, 0, 0, 0)),
            pl.BlockSpec((high, 8, hidden), lambda t: (0, 0, 0)),
        ],
        out_specs=(
            rows_of(rows_g), rows_of(rows_e), rows_of(rows_m),
            turned_spec, turned_spec, turned_spec,
            pl.BlockSpec((hidden,), lambda t: (0,)), rows_of(hidden),
        ),
        out_shape=(
            sds((rows_g, width), BF), sds((rows_e, width), BF), sds((rows_m, width), BF),
            sds((width, hidden), F32), sds((width, hidden), F32), sds((width, hidden), F32),
            sds((hidden,), F32), sds((hidden, width), F32),
        ),
        compiler_params=pltpu.CompilerParams(dimension_semantics=("arbitrary",)),
    )(
        grad_grid, grid_in, grad_edge, edge_in, mesh_own, mesh_in,
        out.reshape((2, n) + blocks), bias_out,
    )
    return grad_grid, grad_edge, grad_mesh, gwg, gwm, gwe, gbias, gwo


def solution(mesh):
    rows = P(("band", "chan"), None)
    return jax.shard_map(
        body,
        mesh=mesh,
        in_specs=(
            rows, rows, rows, rows,
            P(None, "chan"), P(None, "chan"), P(None, "chan"), P("chan"), P("chan", None),
            P("band"), P("band"), P("band"),
        ),
        out_specs=(
            rows, rows, rows,
            P(None, "chan"), P(None, "chan"), P(None, "chan"), P("chan"), P("chan", None),
        ),
        check_vma=False,
    )
```

profile of v0, /device:TPU:0, one launch (start us, length us, event | category | flops | bytes accessed | tf_op | source)
XLA Modules:
  0.0 91.0 jit_solution(18174978674188638702)
XLA Ops:
  1.3 1.3 %reshape.31.sender = s32[2,1,1152]{2,1,0:T(1,128)} reshape(s32[2304]{0:T(1024)} %param.21) | data formatting | bytes 18432 | tf_op jit(solution)/shard_map/reshape | solution.py:383
  2.6 1.3 %reshape.32.receiver = s32[2,1,1152]{2,1,0:T(1,128)} reshape(s32[2304]{0:T(1024)} %param.22) | data formatting | bytes 18432 | tf_op jit(solution)/shard_map/reshape | solution.py:383
  3.9 23.0 %shard_map.179 = (bf16[576,512]{1,0:T(8,128)(2,1)}, bf16[1152,512]{1,0:T(8,128)(2,1)}, bf16[3,2,2,160,512]{4,3,2,1,0:T(8,128)(2,1)}) custom-call(bf16[576,512]{1,0:T(8,128)(2,1)} %grid.3, bf16[1152,512]{1,0:T(8,128)(2,1)} %edge.3, bf16[160,512]{1,0:T(8,128)(2,1)} %mesh.1, bf16[160,512]{1,0:T(8,128)(2,1)} %cot.1), custom_call_target="tpu_custom_call" | custom-call | tf_op jit(solution)/shard_map/pallas_call | solution.py:327
  26.9 20.2 %shard_map.180 = (bf16[2304,512]{1,0:T(8,128)(2,1)}, bf16[1152,512]{1,0:T(8,128)(2,1)}, bf16[960,256]{1,0:T(8,128)(2,1)}, bf16[2,16,2,16,512]{4,3,2,1,0:T(8,128)(2,1)}, f32[8,256]{1,0:T(8,128)}) custom-call(s32[1]{0:T(128)S(6)} %copy.20.used, bf16[576,512]{1,0:T(8,128)(2,1)} %grid.3, bf16[576,512]{1,0:T(8,128)(2,1)} %get-tuple-element.22.grid_oth, ...), custom_call_target="tpu_custom_call" | custom-call | tf_op jit(solution)/shard_map/pallas_call | solution.py:349
  47.1 39.9 %shard_map.181 = (bf16[1152,512]{1,0:T(8,128)(2,1)}, bf16[576,512]{1,0:T(8,128)(2,1)}, bf16[160,512]{1,0:T(8,128)(2,1)}, bf16[160,512]{1,0:T(8,128)(2,1)}, bf16[...) custom-call(bf16[2304,512]{1,0:T(8,128)(2,1)} %get-tuple-element.26.grad_edge.edge_own, ...), custom_call_target="tpu_custom_call" | custom-call | tf_op jit(solution)/shard_map/pallas_call | solution.py:387
  87.0 4.0 %shard_map.182 = (bf16[576,512]{1,0:T(8,128)(2,1)}, bf16[1152,512]{1,0:T(8,128)(2,1)}, bf16[160,512]{1,0:T(8,128)(2,1)}, f32[512,256]{1,0:T(8,128)}, f32[512,256...) custom-call(bf16[1152,512]{1,0:T(8,128)(2,1)} %get-tuple-element.25.grad_grid.grid_own, ...), custom_call_target="tpu_custom_call" | custom-call | tf_op jit(solution)/shard_map/pallas_call | solution.py:414
where the time goes:
time: 91.3 us; the launch traced here: 91 us
  Pallas kernels  87.1 us (95%)
  local copies, waits for them, and re-layouts  2.63 us (3%)
  between operations  1.3 us (1%)
    pallas_call x1, Pallas kernels, body(): pl.pallas_call(functools.partial(reduce_kernel, low, high), out_shape=(sd...  39.9 us
    pallas_call x1, Pallas kernels, body(): pl.pallas_call(functools.partial(gather_kernel, n), out_shape=(sds(grid_l...  23 us
    pallas_call x1, Pallas kernels, body(): pl.pallas_call(functools.partial(main_kernel, tiles, own_m), grid=(tiles,...  20.2 us
    pallas_call x1, Pallas kernels, body(): pl.pallas_call(final_kernel, grid=(2,), in_specs=[rows_of(rows_g), rows_o...  3.97 us

commit v1 on v0

v1 whole, which is shorter than its diff:
```python
import functools

import jax
import jax.numpy as jnp
from jax import lax
from jax.experimental import pallas as pl
from jax.experimental.pallas import tpu as pltpu
from jax.sharding import PartitionSpec as P

BF = jnp.bfloat16
F32 = jnp.float32
MESH = pl.DeviceIdType.MESH
VMEM = pl.BlockSpec(memory_space=pltpu.VMEM)
ANY = pl.BlockSpec(memory_space=pl.ANY)
NN = (((1,), (0,)), ((), ()))
NT = (((1,), (1,)), ((), ()))
TN = (((0,), (0,)), ((), ()))
WO, WE, WM, WG = range(4)


def mm(a, b, dims=NN):
    return lax.dot_general(a, b, dims, preferred_element_type=F32)


def remote(src, dst, send, recv, device):
    return pltpu.make_async_remote_copy(
        src_ref=src, dst_ref=dst, send_sem=send, recv_sem=recv,
        device_id=device, device_id_type=MESH,
    )


def turned(x):
    return x.astype(F32).T.astype(BF)


def mega_kernel(
    low, high, tile,
    used, grid, edge, mesh, cot, wg, we, wm, wo, bias, sender, receiver,
    edge_out, grid_out, mesh_out, out, bias_out,
    gridv, xv, win, wgv, wev, wmv, wov, biasv, senderv, receiverv,
    wg_t, we_t, s_t, r_t, pg, pm, pre_v, act_v, pc_v, rsum,
    ge_v, ge_in, gg_v, gg_in, rx, rims, gm_v, gm_in,
    gall, in1, sum1, in2, sum2, out1, outv, gb_own, gb_in, gb_sum, gb_all, gb_out,
    local, send, recv, s1, r1, s2, r2, s3, r3, s4, r4, sb, rb, sc, rc,
):
    n = low * high
    me, half = lax.axis_index("band"), lax.axis_index("chan")
    mine, plane = lax.rem(me, low), me // low
    up, down = lax.rem(me + 1, n), lax.rem(me + n - 1, n)
    partner = {"band": me, "chan": 1 - half}
    above, below = {"band": up, "chan": half}, {"band": down, "chan": half}
    rows_g, width = grid.shape
    rows_e, rows_m = edge.shape[0], mesh.shape[0]
    hidden = wg.shape[1]
    own_m = 2 * rows_m
    window = 3 * own_m
    padded = r_t.shape[0]
    edges = 2 * rows_e
    tiles = edges // tile

    barrier = pltpu.get_barrier_semaphore()

    def greet(k, carry):
        pl.semaphore_signal(
            barrier, inc=1, device_id={"band": lax.rem(me + k, n), "chan": half},
            device_id_type=MESH)
        return carry
    pl.semaphore_signal(barrier, inc=1, device_id=partner, device_id_type=MESH)
    lax.fori_loop(1, n, greet, 0)

    loads = [
        pltpu.make_async_copy(src, dst, local.at[i])
        for i, (src, dst) in enumerate((
            (mesh, win.at[0, 1, half]), (cot, win.at[1, 1, half]),
            (grid, gridv.at[half]), (edge, xv.at[half]),
            (wg, wgv), (we, wev), (wm, wmv), (wo, wov), (bias, biasv),
            (sender, senderv), (receiver, receiverv),
        ))
    ]
    for copy in loads:
        copy.start()

    def peer(k):
        return {"band": plane * low + lax.rem(mine + k, low), "chan": half}

    def far(k):
        return {"band": lax.rem(plane + k, high) * low + mine, "chan": half}

    lows, highs = range(1, low), range(1, high)

    def scatter_low(k, w):
        return remote(gall.at[w, lax.rem(mine + k, low)], in1.at[w, k], s1.at[w, k], r1.at[w, k],
                      peer(k))

    def scatter_high(k, w):
        return remote(sum1.at[w, lax.rem(plane + k, high)], in2.at[w, k], s2.at[w, k],
                      r2.at[w, k], far(k))

    def gather_high(k, w):
        return remote(sum2.at[w], out1.at[w, plane], s3.at[w, k], r3.at[w, k], far(k))

    def gather_low(k, w):
        return remote(out1.at[w], out.at[w, mine], s4.at[w, k], r4.at[w, k], peer(k))

    def bias_low(k):
        return remote(gb_own, gb_in.at[mine], sb.at[k], rb.at[k], peer(k))

    def bias_high(k):
        return remote(gb_sum, gb_all.at[plane], sc.at[k], rc.at[k], far(k))

    def offer(w, value):
        gall[w] = value.reshape(gall.shape[1:]).astype(BF)
        for k in lows:
            scatter_low(k, w).start()

    def reduce_low(w):
        for k in lows:
            scatter_low(k, w).wait()
        total = gall[w, mine].astype(F32)
        for k in lows:
            total = total + in1[w, k].astype(F32)
        sum1[w] = total.astype(BF)
        for k in highs:
            scatter_high(k, w).start()

    def reduce_high(w):
        for k in highs:
            scatter_high(k, w).wait()
        total = sum1[w, plane].astype(F32)
        for k in highs:
            total = total + in2[w, k].astype(F32)
        sum2[w] = total.astype(BF)
        for k in highs:
            gather_high(k, w).start()
        out1[w, plane] = sum2[w]

    own_out = [
        pltpu.make_async_copy(out1.at[w], out.at[w, mine], local.at[16 + w]) for w in range(4)
    ]

    def spread(w):
        for k in highs:
            gather_high(k, w).wait()
        for k in lows:
            gather_low(k, w).start()
        own_out[w].start()

    for copy in loads:
        copy.wait()
    wg_t[...] = turned(wgv[...])
    we_t[...] = turned(wev[...])
    bcol = jnp.broadcast_to(biasv[...].reshape(1, hidden), (128, hidden)).T[:, :1]
    pl.semaphore_wait(barrier, n)

    def to_side(which, side, device, i):
        src = win.at[which, 1, half]
        return remote(src, win.at[which, side, half], send.at[i], recv.at[i], device)

    def swap(ref, i):
        return remote(ref.at[half], ref.at[half], send.at[i], recv.at[i], partner)

    mesh_up, mesh_down = to_side(0, 0, above, 0), to_side(0, 2, below, 1)
    cot_up, cot_down = to_side(1, 0, above, 2), to_side(1, 2, below, 3)
    grid_swap, edge_swap = swap(gridv, 4), swap(xv, 5)
    mesh_swap, cot_swap = swap(win.at[0, 1], 6), swap(win.at[1, 1], 7)
    for copy in (mesh_up, mesh_down, grid_swap, edge_swap, mesh_swap, cot_up, cot_down, cot_swap):
        copy.start()

    def pass_on(which, side, i):
        return swap(win.at[which, side], i)

    mesh_on = (pass_on(0, 0, 8), pass_on(0, 2, 9))
    cot_on = (pass_on(1, 0, 10), pass_on(1, 2, 11))

    band_row, mesh_row = me * (2 * rows_g), (me - 1) * own_m
    cuts = [slice(t * tile, (t + 1) * tile) for t in range(tiles)]
    for cut in cuts:
        from_row = senderv[cut].reshape(1, tile) - band_row
        to_row = receiverv[cut].reshape(1, tile) - mesh_row
        s_t[:, cut] = jnp.where(
            lax.broadcasted_iota(jnp.int32, (2 * rows_g, tile), 0) == from_row, 1.0, 0.0
        ).astype(BF)
        r_t[:, cut] = jnp.where(
            lax.broadcasted_iota(jnp.int32, (padded, tile), 0) == to_row, 1.0, 0.0
        ).astype(BF)

    grid_swap.wait()
    grid_all = lambda: gridv[...].reshape(2 * rows_g, width)
    pg[...] = mm(wg_t[...], grid_all(), NT).astype(BF)
    edge_swap.wait()
    x_all = lambda: xv[...].reshape(edges, width)
    for cut in cuts:
        pre_v[:, cut] = mm(pg[...], s_t[:, cut]) + mm(we_t[...], x_all()[cut], NT) + bcol

    def nodes(which):
        rows_in = win[which].reshape(window, width)
        if padded > window:
            rows_in = jnp.concatenate(
                [rows_in, jnp.zeros((padded - window, width), BF)], axis=0)
        return rows_in

    mesh_up.wait()
    mesh_on[0].start()
    mesh_down.wait()
    mesh_on[1].start()
    mesh_swap.wait()
    for copy in mesh_on:
        copy.wait()
    pm[...] = mm(nodes(0), wmv[...]).T.astype(BF)
    count = used[0]
    alive = [
        jnp.where(lax.broadcasted_iota(jnp.int32, (1, tile), 1) + t * tile < count, 1.0, 0.0)
        for t in range(tiles)
    ]
    for t, cut in enumerate(cuts):
        pre = pre_v[:, cut] + mm(pm[...], r_t[:, cut])
        sig = jax.nn.sigmoid(pre)
        act_v[:, cut] = (pre * sig * alive[t]).astype(BF)
        pre_v[:, cut] = sig * (1.0 + pre * (1.0 - sig)) * alive[t]
    rsum[...] = mm(act_v[...], r_t[...], NT).astype(BF)

    cot_up.wait()
    cot_on[0].start()
    cot_down.wait()
    cot_on[1].start()
    cot_swap.wait()
    for copy in cot_on:
        copy.wait()
    offer(WO, mm(rsum[...], nodes(1)))
    pm[...] = mm(wov[...], nodes(1), NT).astype(BF)
    for cut in cuts:
        pc_v[:, cut] = (mm(pm[...], r_t[:, cut]) * pre_v[:, cut]).astype(BF)
    offer(WE, mm(pc_v[...], x_all()))

    gb = jnp.zeros((hidden, 128), F32)
    for k in range(edges // 128):
        gb = gb + pc_v[:, k * 128:(k + 1) * 128].astype(F32)
    gb_own[...] = jnp.broadcast_to(jnp.sum(gb.T, axis=0, keepdims=True), gb_own.shape)
    for k in lows:
        bias_low(k).start()

    sr = mm(pc_v[...], r_t[...], NT)
    offer(WM, mm(sr.astype(BF), nodes(0)))
    rx[...] = sr.T[:window].astype(BF).reshape(rx.shape)
    raise_up = remote(rx.at[2], rims.at[0], send.at[12], recv.at[12], above)
    lower = remote(rx.at[0], rims.at[1], send.at[13], recv.at[13], below)

    sg = mm(pc_v[...], s_t[...], NT).astype(BF)
    offer(WG, mm(sg, grid_all()))
    raise_up.start()
    lower.start()
    reduce_low(WO)
    gg_v[...] = mm(sg, wg_t[...], TN).astype(BF).reshape(gg_v.shape)
    grid_copy = remote(gg_v.at[1 - half], gg_in, send.at[14], recv.at[14], partner)
    grid_copy.start()
    reduce_low(WE)
    ge_v[...] = mm(pc_v[...], we_t[...], TN).astype(BF).reshape(ge_v.shape)
    edge_copy = remote(ge_v.at[1 - half], ge_in, send.at[15], recv.at[15], partner)
    edge_copy.start()

    for k in lows:
        bias_low(k).wait()
    gb_in[mine] = gb_own[...]
    gb_sum[...] = jnp.sum(gb_in[...], axis=0)
    for k in highs:
        bias_high(k).start()
    reduce_low(WM)
    reduce_high(WO)
    reduce_low(WG)
    reduce_high(WE)

    def settle(copy, own, other, to, i):
        copy.wait()
        own[half] = (own[half].astype(F32) + other[...].astype(F32)).astype(BF)
        done = pltpu.make_async_copy(own.at[half], to, local.at[i])
        done.start()
        return done

    grid_done = settle(grid_copy, gg_v, gg_in, grid_out, 11)
    spread(WO)
    edge_done = settle(edge_copy, ge_v, ge_in, edge_out, 12)
    reduce_high(WM)
    spread(WE)
    raise_up.wait()
    lower.wait()
    total = (rx[1].astype(F32) + rims[0].astype(F32) + rims[1].astype(F32)).astype(BF)
    gm_v[...] = mm(total, wmv[...], NT).astype(BF).reshape(gm_v.shape)
    mesh_copy = remote(gm_v.at[1 - half], gm_in, send.at[16], recv.at[16], partner)
    mesh_copy.start()
    reduce_high(WG)
    spread(WM)
    for k in highs:
        bias_high(k).wait()
    gb_all[plane] = gb_sum[...]
    gb_out[...] = jnp.sum(gb_all[...], axis=0)
    bias_done = pltpu.make_async_copy(gb_out, bias_out, local.at[14])
    bias_done.start()
    mesh_done = settle(mesh_copy, gm_v, gm_in, mesh_out, 13)
    spread(WG)
    for copy in (grid_done, edge_done, bias_done, mesh_done, *own_out):
        copy.wait()
    for w in range(4):
        for k in lows:
            gather_low(k, w).wait()


def final_kernel(
    grid_sum, edge_sum, mesh_sum, out, bias_sum,
    grad_grid, grad_edge, grad_mesh, gwg, gwm, gwe, gbias, gwo,
):
    grad_grid[...] = grid_sum[...]
    grad_edge[...] = edge_sum[...]
    grad_mesh[...] = mesh_sum[...]
    full = lambda w: out[w].astype(F32).reshape(gwo.shape)
    gwg[...] = full(WG).T
    gwe[...] = full(WE).T
    gwm[...] = full(WM).T
    gwo[...] = full(WO)
    gbias[...] = bias_sum[...][0]


def body(
    grid_latent,
    edge_latent,
    mesh_latent,
    mesh_cotangent,
    w_grid,
    w_mesh,
    w_edge,
    bias,
    w_out,
    senders,
    receivers,
    edge_count,
):
    n = lax.axis_size("band")
    rows_g, width = grid_latent.shape
    rows_e = edge_latent.shape[0]
    rows_m = mesh_latent.shape[0]
    hidden = w_grid.shape[1]
    own_m = 2 * rows_m
    edges = 2 * rows_e
    sds = jax.ShapeDtypeStruct
    dma = pltpu.SemaphoreType.DMA
    vm = pltpu.VMEM

    tile = max(d for d in range(128, 1025, 128) if edges % d == 0)
    padded = -(-3 * own_m // 256) * 256
    low = 1
    while low * low < n:
        low *= 2
    high = n // low
    rows_c = hidden // n
    piece = (rows_c, width)
    grid_sum, edge_sum, mesh_sum, out, bias_sum = (lambda r: (r[1], r[0], r[2], r[3], r[4]))(
        pl.pallas_call(
            functools.partial(mega_kernel, low, high, tile),
            out_shape=(
                sds((rows_e, width), BF), sds((rows_g, width), BF), sds((rows_m, width), BF),
                sds((4, low, high) + piece, BF), sds((8, hidden), F32),
            ),
            in_specs=[pl.BlockSpec(memory_space=pltpu.SMEM)] + [ANY] * 11,
            out_specs=(ANY,) * 5,
            scratch_shapes=[
                vm((2, rows_g, width), BF), vm((2, rows_e, width), BF),
                vm((2, 3, 2, rows_m, width), BF),
                vm((width, hidden), BF), vm((width, hidden), BF), vm((width, hidden), BF),
                vm((hidden, width), BF), vm((hidden,), F32),
                vm((edges,), jnp.int32), vm((edges,), jnp.int32),
                vm((hidden, width), BF), vm((hidden, width), BF),
                vm((2 * rows_g, edges), BF), vm((padded, edges), BF),
                vm((hidden, 2 * rows_g), BF), vm((hidden, padded), BF),
                vm((hidden, edges), F32), vm((hidden, edges), BF), vm((hidden, edges), BF),
                vm((hidden, padded), BF),
                vm((2, rows_e, width), BF), vm((rows_e, width), BF),
                vm((2, rows_g, width), BF), vm((rows_g, width), BF),
                vm((3, own_m, hidden), BF), vm((2, own_m, hidden), BF),
                vm((2, rows_m, width), BF), vm((rows_m, width), BF),
                vm((4, low, high) + piece, BF), vm((4, low, high) + piece, BF),
                vm((4, high) + piece, BF), vm((4, high) + piece, BF), vm((4,) + piece, BF),
                vm((4, high) + piece, BF), vm((8, 128), F32),
                vm((8, hidden), F32), vm((low, 8, hidden), F32), vm((8, hidden), F32),
                vm((high, 8, hidden), F32), vm((8, hidden), F32),
                dma((20,)), dma((17,)), dma((17,)),
                dma((4, low)), dma((4, low)), dma((4, high)), dma((4, high)),
                dma((4, high)), dma((4, high)), dma((4, low)), dma((4, low)),
                dma((low,)), dma((low,)), dma((high,)), dma((high,)),
            ],
            compiler_params=pltpu.CompilerParams(
                collective_id=0, has_side_effects=True, vmem_limit_bytes=60 * 2**20),
        )(
            edge_count, grid_latent, edge_latent, mesh_latent, mesh_cotangent,
            w_grid, w_edge, w_mesh, w_out, bias, senders, receivers,
        )
    )

    rows_of = lambda rows: pl.BlockSpec((rows // 2, width), lambda t: (t, 0))
    turned_spec = pl.BlockSpec((width, hidden // 2), lambda t: (0, t))
    return pl.pallas_call(
        final_kernel,
        grid=(2,),
        in_specs=[
            rows_of(rows_g), rows_of(rows_e), rows_of(rows_m),
            pl.BlockSpec((4, n // 2) + piece, lambda t: (0, t, 0, 0)),
            pl.BlockSpec((8, hidden), lambda t: (0, 0)),
        ],
        out_specs=(
            rows_of(rows_g), rows_of(rows_e), rows_of(rows_m),
            turned_spec, turned_spec, turned_spec,
            pl.BlockSpec((hidden,), lambda t: (0,)), rows_of(hidden),
        ),
        out_shape=(
            sds((rows_g, width), BF), sds((rows_e, width), BF), sds((rows_m, width), BF),
            sds((width, hidden), F32), sds((width, hidden), F32), sds((width, hidden), F32),
            sds((hidden,), F32), sds((hidden, width), F32),
        ),
        compiler_params=pltpu.CompilerParams(dimension_semantics=("arbitrary",)),
    )(grid_sum, edge_sum, mesh_sum, out.reshape((4, n) + piece), bias_sum)


def solution(mesh):
    rows = P(("band", "chan"), None)
    return jax.shard_map(
        body,
        mesh=mesh,
        in_specs=(
            rows, rows, rows, rows,
            P(None, "chan"), P(None, "chan"), P(None, "chan"), P("chan"), P("chan", None),
            P("band"), P("band"), P("band"),
        ),
        out_specs=(
            rows, rows, rows,
            P(None, "chan"), P(None, "chan"), P(None, "chan"), P("chan"), P("chan", None),
        ),
        check_vma=False,
    )
```

time: 91.3 us -> 64.7 us (0.71)
  Pallas kernels: 87.1 us -> 63.1 us
  local copies, waits for them, and re-layouts: 2.63 us -> 0 us
    pallas_call x3 -> x1, Pallas kernels: 83.1 us -> 59.6 us  [body(): pl.pallas_call(functools.partial(mega_kernel, low, high, tile), out_shape...]
    reshape x2 -> x0, local copies, waits for them, and re-layouts: 2.63 us -> none  [the longest x1 1.32 us: body(): senders.reshape(tiles, 1, tile)]
where the time goes in v1:
time: 64.7 us; the launch traced here: 64.5 us
  Pallas kernels  63.1 us (98%)
  between operations  1.45 us (2%)
    pallas_call x1, Pallas kernels, body(): pl.pallas_call(functools.partial(mega_kernel, low, high, tile), out_shape...  59.6 us
    pallas_call x1, Pallas kernels, body(): pl.pallas_call(final_kernel, grid=(2,), in_specs=[rows_of(rows_g), rows_o...  3.46 us

profile of v1, /device:TPU:0, one launch (start us, length us, event | category | flops | bytes accessed | tf_op | source)
XLA Modules:
  0.0 64.5 jit_solution(3766669657949975215)
XLA Ops:
  1.3 59.6 %shard_map.179 = (bf16[1152,512]{1,0:T(8,128)(2,1)}, bf16[576,512]{1,0:T(8,128)(2,1)}, bf16[160,512]{1,0:T(8,128)(2,1)}, bf16[4,4,4,16,512]{4,3,2,1,0:T(8,128)(2,1)}, f32[8,256]{1,0:T(8,128)}) custom-call(s32[1]{0:T(128)S(6)} %copy.20.used, bf16[576,512]{1,0:T(8,128)(2,1)} %grid.1, bf16[1152,512]{1,0:T(8,128)(2,1)} %edge.1, bf16[160,512]{1,0:T(8,128)(2,1)} %mesh.1, ...), custom_call_target="tpu_custom_call" | custom-call | tf_op jit(solution)/shard_map/pallas_call | solution.py:356
  60.9 3.5 %shard_map.180 = (bf16[576,512]{1,0:T(8,128)(2,1)}, bf16[1152,512]{1,0:T(8,128)(2,1)}, bf16[160,512]{1,0:T(8,128)(2,1)}, f32[512,256]{1,0:T(8,128)}, f32[512,256...) custom-call(bf16[576,512]{1,0:T(8,128)(2,1)} %get-tuple-element.13.grid_sum, ...), custom_call_target="tpu_custom_call" | custom-call | tf_op jit(solution)/shard_map/pallas_call | solution.py:399

commit v2 on v1

v2 whole, which is shorter than its diff:
```python
import functools

import jax
import jax.numpy as jnp
from jax import lax
from jax.experimental import pallas as pl
from jax.experimental.pallas import tpu as pltpu
from jax.sharding import PartitionSpec as P

BF = jnp.bfloat16
F32 = jnp.float32
MESH = pl.DeviceIdType.MESH
VMEM = pl.BlockSpec(memory_space=pltpu.VMEM)
ANY = pl.BlockSpec(memory_space=pl.ANY)
NN = (((1,), (0,)), ((), ()))
NT = (((1,), (1,)), ((), ()))
TN = (((0,), (0,)), ((), ()))
WO, WE, WM, WG = range(4)
STAGE = (5.0, 4.2, 4.2, 5.0)


def mm(a, b, dims=NN):
    return lax.dot_general(a, b, dims, preferred_element_type=F32)


def remote(src, dst, send, recv, device):
    return pltpu.make_async_remote_copy(
        src_ref=src, dst_ref=dst, send_sem=send, recv_sem=recv,
        device_id=device, device_id_type=MESH,
    )


def turned(x):
    return x.astype(F32).T.astype(BF)


def mega_kernel(
    tile,
    used, grid, edge, mesh, cot, wg, we, wm, wo, bias, sender, receiver,
    edge_out, grid_out, mesh_out, out, bias_out,
    gridv, xv, win, wgv, wev, wmv, wov, biasv, senderv, receiverv,
    wg_t, we_t, s_t, r_t, pg, pm, pre_v, act_v, pc_v, rsum,
    ge_v, ge_in, gg_v, gg_in, rx, rims, rxs, gm_v, gm_in,
    gall, in1, sum1, in2, sum2, out1, gb_own, gb_in, gb_sum, gb_all, gb_out,
    local, send, recv, wins, xr, fr, pr, qr, ws, wr,
):
    n, half = lax.axis_size("band"), lax.axis_index("chan")
    me = lax.axis_index("band")
    cuts_w, high = gall.shape[1], gall.shape[3]
    mine, plane = lax.rem(me, 4), me // 4
    odd = lax.rem(me, 2)
    pair = me + 1 - 2 * odd
    onward = lax.rem(me + 2 - 4 * odd + n, n)
    backward = lax.rem(me - 2 + 4 * odd + n, n)
    at = lambda band: {"band": band, "chan": half}
    partner = {"band": me, "chan": 1 - half}
    rows_g, width = grid.shape
    rows_e, rows_m = edge.shape[0], mesh.shape[0]
    hidden = wg.shape[1]
    own_m = 2 * rows_m
    window = 3 * own_m
    padded = r_t.shape[0]
    edges = 2 * rows_e
    tiles = edges // tile
    steps = win.shape[3]

    barrier = pltpu.get_barrier_semaphore()

    def greet(k, carry):
        pl.semaphore_signal(
            barrier, inc=1, device_id=at(lax.rem(me + k, n)), device_id_type=MESH)
        return carry
    pl.semaphore_signal(barrier, inc=1, device_id=partner, device_id_type=MESH)
    lax.fori_loop(1, n, greet, 0)

    loads = [
        pltpu.make_async_copy(src, dst, local.at[i])
        for i, (src, dst) in enumerate((
            (mesh.reshape(win.shape[3:]), win.at[0, 1, half]),
            (cot.reshape(win.shape[3:]), win.at[1, 1, half]),
            (grid, gridv.at[half]), (edge, xv.at[half]),
            (sender, senderv), (receiver, receiverv),
            (wg, wgv), (we, wev), (wm, wmv), (wo, wov), (bias, biasv),
        ))
    ]
    for copy in loads:
        copy.start()

    def each(lo, hi, fn):
        if hi - lo <= 8:
            for k in range(lo, hi):
                fn(k)
        else:
            lax.fori_loop(lo, hi, lambda k, carry: (fn(k), carry)[1], 0)

    def swap(ref, s, r):
        return remote(ref.at[half], ref.at[half], s, r, partner)

    def pair_copy(v, i):
        return remote(win.at[v, 1, half, i], win.at[v, 2 * odd, half, i],
                      wins.at[v], xr.at[v, i], at(pair))

    def onward_copy(v, i):
        return remote(win.at[v, 2 - 2 * odd, half, i], win.at[v, 2 * odd, half, i],
                      wins.at[v], fr.at[v, i], at(onward))

    def pair_share(v, i):
        ref = win.at[v, 2 - 2 * odd, half, i]
        return remote(ref, ref, wins.at[v], pr.at[v], partner)

    def onward_share(v, i):
        ref = win.at[v, 2 * odd, half, i]
        return remote(ref, ref, wins.at[v], qr.at[v], partner)

    def pass_pair(v, i):
        pair_copy(v, i).wait_recv()
        onward_copy(v, i).start()
        pair_share(v, i).start()

    def pass_onward(v, i):
        onward_copy(v, i).wait_recv()
        onward_share(v, i).start()

    def shared(v):
        for side, sem in ((2 - 2 * odd, pr), (2 * odd, qr)):
            ref = win.at[v, side, 1 - half]
            remote(ref, ref, wins.at[v], sem.at[v], partner).wait_recv()

    grid_swap, edge_swap = swap(gridv, send.at[0], recv.at[0]), swap(xv, send.at[1], recv.at[1])
    mesh_swap = swap(win.at[0, 1], send.at[2], recv.at[2])
    cot_swap = swap(win.at[1, 1], send.at[3], recv.at[3])

    for copy in loads[:4]:
        copy.wait()
    pl.semaphore_wait(barrier, n)
    for v in (0, 1):
        for i in range(steps):
            pair_copy(v, i).start()
    for copy in (grid_swap, mesh_swap, edge_swap, cot_swap):
        copy.start()
    for copy in loads[4:]:
        copy.wait()
    wg_t[...] = turned(wgv[...])
    we_t[...] = turned(wev[...])
    bcol = jnp.broadcast_to(biasv[...].reshape(1, hidden), (128, hidden)).T[:, :1]

    band_row, mesh_row = me * (2 * rows_g), (me - 1) * own_m
    cuts = [slice(t * tile, (t + 1) * tile) for t in range(tiles)]
    for cut in cuts:
        from_row = senderv[cut].reshape(1, tile) - band_row
        to_row = receiverv[cut].reshape(1, tile) - mesh_row
        s_t[:, cut] = jnp.where(
            lax.broadcasted_iota(jnp.int32, (2 * rows_g, tile), 0) == from_row, 1.0, 0.0
        ).astype(BF)
        r_t[:, cut] = jnp.where(
            lax.broadcasted_iota(jnp.int32, (padded, tile), 0) == to_row, 1.0, 0.0
        ).astype(BF)

    todo = [(v, i) for v in (0, 1) for i in range(steps)]
    pass_pair(*todo.pop(0))
    grid_swap.wait()
    grid_all = lambda: gridv[...].reshape(2 * rows_g, width)
    pg[...] = mm(wg_t[...], grid_all(), NT).astype(BF)
    edge_swap.wait()
    x_all = lambda: xv[...].reshape(edges, width)
    for cut in cuts:
        pre_v[:, cut] = mm(pg[...], s_t[:, cut]) + mm(we_t[...], x_all()[cut], NT) + bcol
        if todo:
            pass_pair(*todo.pop(0))
    for item in todo:
        pass_pair(*item)

    def nodes(which):
        rows_in = win[which].reshape(window, width)
        if padded > window:
            rows_in = jnp.concatenate(
                [rows_in, jnp.zeros((padded - window, width), BF)], axis=0)
        return rows_in

    for i in range(steps):
        pass_onward(0, i)
    mesh_swap.wait()
    shared(0)
    pm[...] = mm(nodes(0), wmv[...]).T.astype(BF)
    count = used[0]
    alive = [
        jnp.where(lax.broadcasted_iota(jnp.int32, (1, tile), 1) + t * tile < count, 1.0, 0.0)
        for t in range(tiles)
    ]
    later = list(range(steps))
    for t, cut in enumerate(cuts):
        pre = pre_v[:, cut] + mm(pm[...], r_t[:, cut])
        sig = jax.nn.sigmoid(pre)
        act_v[:, cut] = (pre * sig * alive[t]).astype(BF)
        pre_v[:, cut] = sig * (1.0 + pre * (1.0 - sig)) * alive[t]
        if t >= 1 and later:
            pass_onward(1, later.pop(0))
    rsum[...] = mm(act_v[...], r_t[...], NT).astype(BF)

    for i in later:
        pass_onward(1, i)
    cot_swap.wait()
    shared(1)

    far = lambda k: lax.rem(plane + k, high)
    near = lambda k: lax.rem(mine + k, 4)
    peer = lambda k: at(plane * 4 + near(k))
    distant = lambda k: at(far(k) * 4 + mine)

    def to(stage, w, c, src, dst, device):
        remote(src, dst, ws.at[w, c], wr.at[stage, w, c], device).start()

    def landed(stage, w, c, ref):
        remote(ref, ref, ws.at[w, c], wr.at[stage, w, c], partner).wait()

    def offer(w, value):
        part = width // cuts_w
        for c in range(cuts_w):
            gall[w, c] = value[:, c * part:(c + 1) * part].reshape(gall.shape[2:]).astype(BF)
            for k in (1, 3, 2):
                to(0, w, c, gall.at[w, c, near(k)], in1.at[w, c, k], peer(k))

    def step1(w, c):
        landed(0, w, c, in1.at[w, c, pl.ds(1, 3)])
        total = gall[w, c, mine].astype(F32)
        for k in range(1, 4):
            total = total + in1[w, c, k].astype(F32)
        sum1[w, c] = total.astype(BF)
        each(1, high, lambda k: to(1, w, c, sum1.at[w, c, far(k)], in2.at[w, c, k], distant(k)))

    def step2(w, c):
        landed(1, w, c, in2.at[w, c, pl.ds(1, high - 1)])
        in2[w, c, 0] = sum1[w, c, plane]
        sum2[w, c] = jnp.sum(in2[w, c].astype(F32), axis=0).astype(BF)
        each(1, high, lambda k: to(2, w, c, sum2.at[w, c], out1.at[w, c, plane], distant(k)))
        out1[w, c, plane] = sum2[w, c]

    def step3(w, c):
        landed(2, w, c, in2.at[w, c, pl.ds(1, high - 1)])
        for k in (1, 3, 2):
            to(3, w, c, out1.at[w, c], out.at[w, c, mine], peer(k))
        keep(w, c).start()

    def step4(w, c):
        landed(3, w, c, in1.at[w, c, pl.ds(1, 3)])

    def keep(w, c):
        return pltpu.make_async_copy(out1.at[w, c], out.at[w, c, mine], local.at[15])

    stages = ((step1, STAGE[0]), (step2, STAGE[1]), (step3, STAGE[2]), (step4, STAGE[3]))

    def bias_low(k):
        return remote(gb_own, gb_in.at[k], send.at[4], recv.at[4], peer(k))

    def bias_high(k):
        return remote(gb_sum, gb_all.at[k], send.at[5], recv.at[5], distant(k))

    rx_on = [
        remote(rx.at[2 * odd, i], rims.at[0, i], send.at[9 + i], recv.at[9 + i], at(backward))
        for i in (0, 1)
    ]
    rx_pair = [
        remote(rxs.at[i], rims.at[1, i], send.at[11 + i], recv.at[11 + i], at(pair))
        for i in (0, 1)
    ]
    grid_copy = remote(gg_v.at[1 - half], gg_in, send.at[6], recv.at[6], partner)
    edge_copy = remote(ge_v.at[1 - half], ge_in, send.at[7], recv.at[7], partner)
    mesh_copy = remote(gm_v.at[1 - half], gm_in, send.at[8], recv.at[8], partner)

    def settle(copy, own, other, to, i):
        copy.wait()
        own[half] = (own[half].astype(F32) + other[...].astype(F32)).astype(BF)
        pltpu.make_async_copy(own.at[half], to, local.at[i]).start()

    grid_sum = (grid_copy, gg_v, gg_in, grid_out, 11)
    edge_sum = (edge_copy, ge_v, ge_in, edge_out, 12)
    mesh_sum = (mesh_copy, gm_v, gm_in, mesh_out, 13)
    bias_done = pltpu.make_async_copy(gb_out, bias_out, local.at[14])

    def rx_step1(i):
        rx_on[i].wait()
        rxs[i] = (rx[2 - 2 * odd, i].astype(F32) + rims[0, i].astype(F32)).astype(BF)
        rx_pair[i].start()

    def rx_step2():
        for copy in rx_pair:
            copy.wait()
        total = (rx[1].astype(F32) + rims[1].astype(F32)).astype(BF).reshape(own_m, hidden)
        gm_v[...] = mm(total, wmv[...], NT).astype(BF).reshape(gm_v.shape)
        mesh_copy.start()

    def bias_step1():
        ref = gb_in.at[pl.ds(1, 3)]
        remote(ref, ref, send.at[4], recv.at[4], partner).wait()
        gb_in[0] = gb_own[...]
        gb_sum[...] = jnp.sum(gb_in[...], axis=0)
        each(1, high, lambda k: bias_high(k).start())

    def bias_step2():
        ref = gb_all.at[pl.ds(1, high - 1)]
        remote(ref, ref, send.at[5], recv.at[5], partner).wait()
        gb_all[0] = gb_sum[...]
        gb_out[...] = jnp.sum(gb_all[...], axis=0)
        bias_done.start()

    keepsake = {}

    def make_wo():
        offer(WO, mm(rsum[...], nodes(1)))

    def make_hidden():
        pm[...] = mm(wov[...], nodes(1), NT).astype(BF)
        for cut in cuts:
            pc_v[:, cut] = (mm(pm[...], r_t[:, cut]) * pre_v[:, cut]).astype(BF)

    def make_we():
        offer(WE, mm(pc_v[...], x_all()))

    def make_bias():
        gb = jnp.zeros((hidden, 128), F32)
        for k in range(edges // 128):
            gb = gb + pc_v[:, k * 128:(k + 1) * 128].astype(F32)
        gb_own[...] = jnp.broadcast_to(jnp.sum(gb.T, axis=0, keepdims=True), gb_own.shape)
        for k in range(1, 4):
            bias_low(k).start()

    def make_wm():
        sr = mm(pc_v[...], r_t[...], NT)
        offer(WM, mm(sr.astype(BF), nodes(0)))
        rx[...] = sr.T[:window].astype(BF).reshape(rx.shape)

    def make_wg():
        keepsake["sg"] = mm(pc_v[...], s_t[...], NT).astype(BF)
        offer(WG, mm(keepsake["sg"], grid_all()))

    def make_grid():
        gg_v[...] = mm(keepsake["sg"], wg_t[...], TN).astype(BF).reshape(gg_v.shape)
        grid_copy.start()

    def make_edge():
        ge_v[...] = mm(pc_v[...], we_t[...], TN).astype(BF).reshape(ge_v.shape)
        edge_copy.start()

    PLAN = (
        (8.2, "rx0a", lambda now: rx_on[0].start()),
        (8.2, "rx0b", lambda now: rx_on[1].start()),
        (12.5, "rx1a", lambda now: rx_step1(0)),
        (14.0, "rx1b", lambda now: rx_step1(1)),
        (15.0, "bias1", lambda now: bias_step1()),
        (12.0, "set_grid", lambda now: settle(*grid_sum)),
        (13.0, "set_edge", lambda now: settle(*edge_sum)),
        (18.0, "rx2", lambda now: rx_step2()),
        (20.5, "set_mesh", lambda now: settle(*mesh_sum)),
        (19.0, "bias2", lambda now: bias_step2()),
    )
    events = []

    def plan(time, name, fn):
        events.append((time, len(events), name, fn))

    def chain(time, w, c, stage):
        fn, lasts = stages[stage]

        def run(now):
            fn(w, c)
            if stage < len(stages) - 1:
                chain(max(now, time + lasts), w, c, stage + 1)
        plan(time + lasts, f"s{stage + 1}_{w}{c}", run)

    def due(now):
        while events and min(events)[0] <= now:
            event = min(events)
            events.remove(event)
            event[3](max(now, event[0]) if now < 1e6 else event[0])

    def offered(w):
        return lambda now: [chain(now, w, c, 0) for c in range(cuts_w)]

    now = 0.0
    for name, fn, lasts, after in (
        ("gwo", make_wo, 0.4, offered(WO)),
        ("hid", make_hidden, 1.8, None),
        ("gwe", make_we, 0.8, offered(WE)),
        ("sr", make_wm, 1.7, offered(WM)),
        ("sg", make_wg, 2.7, offered(WG)),
        ("bias", make_bias, 0.2, None),
        ("gradgrid", make_grid, 0.5, None),
        ("gradedge", make_edge, 0.8, None),
    ):
        due(now)
        fn()
        now += lasts
        if after is not None:
            after(now)
    for time, name, fn in PLAN:
        plan(time, name, fn)
    due(1e9)
    for copy, own, _, to, i in (grid_sum, edge_sum, mesh_sum):
        pltpu.make_async_copy(own.at[half], to, local.at[i]).wait()
    bias_done.wait()
    kept = out1.at[...]
    pltpu.make_async_copy(kept, kept, local.at[15]).wait()
    for v in (0, 1):
        ref = win.at[v, pl.ds(0, 2)]
        remote(ref, ref, wins.at[v], pr.at[v], partner).wait_send()


def final_kernel(
    grid_sum, edge_sum, mesh_sum, out, bias_sum,
    grad_grid, grad_edge, grad_mesh, gwg, gwm, gwe, gbias, gwo,
):
    grad_grid[...] = grid_sum[...]
    grad_edge[...] = edge_sum[...]
    grad_mesh[...] = mesh_sum[...]
    cuts = range(out.shape[1])
    full = lambda w: jnp.concatenate(
        [out[w, c].astype(F32).reshape(gwo.shape[0], -1) for c in cuts], axis=1)
    gwg[...] = full(WG).T
    gwe[...] = full(WE).T
    gwm[...] = full(WM).T
    gwo[...] = full(WO)
    gbias[...] = bias_sum[...][0]


def body(
    grid_latent,
    edge_latent,
    mesh_latent,
    mesh_cotangent,
    w_grid,
    w_mesh,
    w_edge,
    bias,
    w_out,
    senders,
    receivers,
    edge_count,
):
    n = lax.axis_size("band")
    rows_g, width = grid_latent.shape
    rows_e = edge_latent.shape[0]
    rows_m = mesh_latent.shape[0]
    hidden = w_grid.shape[1]
    own_m = 2 * rows_m
    edges = 2 * rows_e
    sds = jax.ShapeDtypeStruct
    dma = pltpu.SemaphoreType.DMA
    vm = pltpu.VMEM

    tile = max(d for d in range(128, 1025, 128) if edges % d == 0)
    padded = -(-3 * own_m // 256) * 256
    high = n // 4
    rows_c = hidden // n
    cuts_w, steps = 2, 2
    piece = (rows_c, width // cuts_w)
    edge_sum, grid_sum, mesh_sum, out, bias_sum = pl.pallas_call(
        functools.partial(mega_kernel, tile),
        out_shape=(
            sds((rows_e, width), BF), sds((rows_g, width), BF), sds((rows_m, width), BF),
            sds((4, cuts_w, 4, high) + piece, BF), sds((8, hidden), F32),
        ),
        in_specs=[pl.BlockSpec(memory_space=pltpu.SMEM)] + [ANY] * 11,
        out_specs=(ANY,) * 5,
        scratch_shapes=[
            vm((2, rows_g, width), BF), vm((2, rows_e, width), BF),
            vm((2, 3, 2, steps, rows_m // steps, width), BF),
            vm((width, hidden), BF), vm((width, hidden), BF), vm((width, hidden), BF),
            vm((hidden, width), BF), vm((hidden,), F32),
            vm((edges,), jnp.int32), vm((edges,), jnp.int32),
            vm((hidden, width), BF), vm((hidden, width), BF),
            vm((2 * rows_g, edges), BF), vm((padded, edges), BF),
            vm((hidden, 2 * rows_g), BF), vm((hidden, padded), BF),
            vm((hidden, edges), F32), vm((hidden, edges), BF), vm((hidden, edges), BF),
            vm((hidden, padded), BF),
            vm((2, rows_e, width), BF), vm((rows_e, width), BF),
            vm((2, rows_g, width), BF), vm((rows_g, width), BF),
            vm((3, 2, rows_m, hidden), BF), vm((2, 2, rows_m, hidden), BF),
            vm((2, rows_m, hidden), BF),
            vm((2, rows_m, width), BF), vm((rows_m, width), BF),
            vm((4, cuts_w, 4, high) + piece, BF), vm((4, cuts_w, 4, high) + piece, BF),
            vm((4, cuts_w, high) + piece, BF), vm((4, cuts_w, high) + piece, BF),
            vm((4, cuts_w) + piece, BF), vm((4, cuts_w, high) + piece, BF),
            vm((8, hidden), F32), vm((4, 8, hidden), F32), vm((8, hidden), F32),
            vm((high, 8, hidden), F32), vm((8, hidden), F32),
            dma((16,)), dma((13,)), dma((13,)),
            dma((2,)), dma((2, steps)), dma((2, steps)), dma((2,)), dma((2,)),
            dma((4, cuts_w)), dma((4, 4, cuts_w)),
        ],
        compiler_params=pltpu.CompilerParams(
            collective_id=0, has_side_effects=True, vmem_limit_bytes=60 * 2**20),
    )(
        edge_count, grid_latent, edge_latent, mesh_latent, mesh_cotangent,
        w_grid, w_edge, w_mesh, w_out, bias, senders, receivers,
    )

    rows_of = lambda rows: pl.BlockSpec((rows // 2, width), lambda t: (t, 0))
    turned_spec = pl.BlockSpec((width, hidden // 2), lambda t: (0, t))
    return pl.pallas_call(
        final_kernel,
        grid=(2,),
        in_specs=[
            rows_of(rows_g), rows_of(rows_e), rows_of(rows_m),
            pl.BlockSpec((4, cuts_w, n // 2) + piece, lambda t: (0, 0, t, 0, 0)),
            pl.BlockSpec((8, hidden), lambda t: (0, 0)),
        ],
        out_specs=(
            rows_of(rows_g), rows_of(rows_e), rows_of(rows_m),
            turned_spec, turned_spec, turned_spec,
            pl.BlockSpec((hidden,), lambda t: (0,)), rows_of(hidden),
        ),
        out_shape=(
            sds((rows_g, width), BF), sds((rows_e, width), BF), sds((rows_m, width), BF),
            sds((width, hidden), F32), sds((width, hidden), F32), sds((width, hidden), F32),
            sds((hidden,), F32), sds((hidden, width), F32),
        ),
        compiler_params=pltpu.CompilerParams(dimension_semantics=("arbitrary",)),
    )(grid_sum, edge_sum, mesh_sum, out.reshape((4, cuts_w, n) + piece), bias_sum)


def solution(mesh):
    rows = P(("band", "chan"), None)
    return jax.shard_map(
        body,
        mesh=mesh,
        in_specs=(
            rows, rows, rows, rows,
            P(None, "chan"), P(None, "chan"), P(None, "chan"), P("chan"), P("chan", None),
            P("band"), P("band"), P("band"),
        ),
        out_specs=(
            rows, rows, rows,
            P(None, "chan"), P(None, "chan"), P(None, "chan"), P("chan"), P("chan", None),
        ),
        check_vma=False,
    )
```

time: 64.7 us -> 62.9 us (0.972)
  Pallas kernels: 63.1 us -> 61.2 us
    pallas_call x1, Pallas kernels: 59.6 us -> 57.8 us  [body(): pl.pallas_call(functools.partial(mega_kernel, tile), out_shape=(sds((rows...]
where the time goes in v2:
time: 62.9 us; the launch traced here: 62.7 us
  Pallas kernels  61.2 us (97%)
  between operations  1.45 us (2%)
    pallas_call x1, Pallas kernels, body(): pl.pallas_call(functools.partial(mega_kernel, tile), out_shape=(sds((rows...  57.8 us
    pallas_call x1, Pallas kernels, body(): pl.pallas_call(final_kernel, grid=(2,), in_specs=[rows_of(rows_g), rows_o...  3.46 us

profile of v2, /device:TPU:0, one launch (start us, length us, event | category | flops | bytes accessed | tf_op | source)
XLA Modules:
  0.0 62.7 jit_solution(16722387520488904857)
XLA Ops:
  1.3 57.8 %shard_map.179 = (bf16[1152,512]{1,0:T(8,128)(2,1)}, bf16[576,512]{1,0:T(8,128)(2,1)}, bf16[160,512]{1,0:T(8,128)(2,1)}, bf16[4,2,4,4,16,256]{5,4,3,2,1,0:T(8,128)(2,1)}, f32[8,256]{1,0:T(8,128)}) custom-call(s32[1]{0:T(128)S(6)} %copy.20.used, bf16[576,512]{1,0:T(8,128)(2,1)} %grid.1, bf16[1152,512]{1,0:T(8,128)(2,1)} %edge.1, bf16[160,512]{1,0:T(8,128)(2,1)} %mesh.1, ...), custom_call_target="tpu_custom_call" | custom-call | tf_op jit(solution)/shard_map/pallas_call | solution.py:456
  59.1 3.5 %shard_map.180 = (bf16[576,512]{1,0:T(8,128)(2,1)}, bf16[1152,512]{1,0:T(8,128)(2,1)}, bf16[160,512]{1,0:T(8,128)(2,1)}, f32[512,256]{1,0:T(8,128)}, f32[512,256...) custom-call(bf16[576,512]{1,0:T(8,128)(2,1)} %get-tuple-element.13.grid_sum, ...), custom_call_target="tpu_custom_call" | custom-call | tf_op jit(solution)/shard_map/pallas_call | solution.py:498

commit v3 on v2

--- a/solution.py
+++ b/solution.py
@@ -16,7 +16,8 @@
 NT = (((1,), (1,)), ((), ()))
 TN = (((0,), (0,)), ((), ()))
 WO, WE, WM, WG = range(4)
-STAGE = (5.0, 4.2, 4.2, 5.0)
+SPLIT = ()
+STAGE = (0.0, 4.2, 4.2, 4.4, 6.0)
 
 
 def mm(a, b, dims=NN):
@@ -39,7 +40,7 @@
     used, grid, edge, mesh, cot, wg, we, wm, wo, bias, sender, receiver,
     edge_out, grid_out, mesh_out, out, bias_out,
     gridv, xv, win, wgv, wev, wmv, wov, biasv, senderv, receiverv,
-    wg_t, we_t, s_t, r_t, pg, pm, pre_v, act_v, pc_v, rsum,
+    wg_t, we_t, s_t, r_t, pg, pm, pc, pre_v, hid_v, act_v, pc_v, sg, rsum,
     ge_v, ge_in, gg_v, gg_in, rx, rims, rxs, gm_v, gm_in,
     gall, in1, sum1, in2, sum2, out1, gb_own, gb_in, gb_sum, gb_all, gb_out,
     local, send, recv, wins, xr, fr, pr, qr, ws, wr,
@@ -48,7 +49,8 @@
     me = lax.axis_index("band")
     cuts_w, high = gall.shape[1], gall.shape[3]
     mine, plane = lax.rem(me, 4), me // 4
-    odd = lax.rem(me, 2)
+    bits = (lax.rem(me, 2), lax.rem(me // 2, 2))
+    odd = bits[0]
     pair = me + 1 - 2 * odd
     onward = lax.rem(me + 2 - 4 * odd + n, n)
     backward = lax.rem(me - 2 + 4 * odd + n, n)
@@ -76,8 +78,8 @@
     loads = [
         pltpu.make_async_copy(src, dst, local.at[i])
         for i, (src, dst) in enumerate((
-            (mesh.reshape(win.shape[3:]), win.at[0, 1, half]),
-            (cot.reshape(win.shape[3:]), win.at[1, 1, half]),
+            (mesh.reshape(win.shape[3:]), win.at[0, 0, half]),
+            (cot.reshape(win.shape[3:]), win.at[1, 0, half]),
             (grid, gridv.at[half]), (edge, xv.at[half]),
             (sender, senderv), (receiver, receiverv),
             (wg, wgv), (we, wev), (wm, wmv), (wo, wov), (bias, biasv),
@@ -97,19 +99,19 @@
         return remote(ref.at[half], ref.at[half], s, r, partner)
 
     def pair_copy(v, i):
-        return remote(win.at[v, 1, half, i], win.at[v, 2 * odd, half, i],
+        return remote(win.at[v, 0, half, i], win.at[v, 1, half, i],
                       wins.at[v], xr.at[v, i], at(pair))
 
     def onward_copy(v, i):
-        return remote(win.at[v, 2 - 2 * odd, half, i], win.at[v, 2 * odd, half, i],
+        return remote(win.at[v, 1, half, i], win.at[v, 2, half, i],
                       wins.at[v], fr.at[v, i], at(onward))
 
     def pair_share(v, i):
-        ref = win.at[v, 2 - 2 * odd, half, i]
+        ref = win.at[v, 1, half, i]
         return remote(ref, ref, wins.at[v], pr.at[v], partner)
 
     def onward_share(v, i):
-        ref = win.at[v, 2 * odd, half, i]
+        ref = win.at[v, 2, half, i]
         return remote(ref, ref, wins.at[v], qr.at[v], partner)
 
     def pass_pair(v, i):
@@ -121,21 +123,22 @@
         onward_copy(v, i).wait_recv()
         onward_share(v, i).start()
 
-    def shared(v):
-        for side, sem in ((2 - 2 * odd, pr), (2 * odd, qr)):
-            ref = win.at[v, side, 1 - half]
-            remote(ref, ref, wins.at[v], sem.at[v], partner).wait_recv()
+    def shared(v, slot):
+        ref, sem = win.at[v, slot, 1 - half], (pr, qr)[slot - 1]
+        remote(ref, ref, wins.at[v], sem.at[v], partner).wait_recv()
 
     grid_swap, edge_swap = swap(gridv, send.at[0], recv.at[0]), swap(xv, send.at[1], recv.at[1])
-    mesh_swap = swap(win.at[0, 1], send.at[2], recv.at[2])
-    cot_swap = swap(win.at[1, 1], send.at[3], recv.at[3])
-
-    for copy in loads[:4]:
+    mesh_swap = swap(win.at[0, 0], send.at[2], recv.at[2])
+    cot_swap = swap(win.at[1, 0], send.at[3], recv.at[3])
+
+    for copy in loads[:2]:
         copy.wait()
     pl.semaphore_wait(barrier, n)
     for v in (0, 1):
         for i in range(steps):
             pair_copy(v, i).start()
+    for copy in loads[2:4]:
+        copy.wait()
     for copy in (grid_swap, mesh_swap, edge_swap, cot_swap):
         copy.start()
     for copy in loads[4:]:
@@ -144,31 +147,44 @@
     we_t[...] = turned(wev[...])
     bcol = jnp.broadcast_to(biasv[...].reshape(1, hidden), (128, hidden)).T[:, :1]
 
-    band_row, mesh_row = me * (2 * rows_g), (me - 1) * own_m
+    block, lanes = 256, 128
+    counted = lax.broadcasted_iota(jnp.int32, (block, lanes), 0).astype(F32).astype(BF)
+    one, zero = jnp.ones((block, lanes), BF), jnp.zeros((block, lanes), BF)
+
+    def mark(ref, row, cut):
+        for base in range(0, ref.shape[0], block):
+            size = min(block, ref.shape[0] - base)
+            local_row = row - base
+            local_row = jnp.where((local_row >= 0) & (local_row < size), local_row, -1)
+            local_row = local_row.astype(F32).astype(BF)
+            for j in range(0, tile, lanes):
+                ref[base:base + size, cut.start + j:cut.start + j + lanes] = jnp.where(
+                    counted[:size] == local_row[:, j:j + lanes], one[:size], zero[:size])
+
+    band_row, mesh_row = me * (2 * rows_g), me * own_m
+    to_below, to_above = own_m * (3 - odd), own_m * odd
     cuts = [slice(t * tile, (t + 1) * tile) for t in range(tiles)]
     for cut in cuts:
         from_row = senderv[cut].reshape(1, tile) - band_row
         to_row = receiverv[cut].reshape(1, tile) - mesh_row
-        s_t[:, cut] = jnp.where(
-            lax.broadcasted_iota(jnp.int32, (2 * rows_g, tile), 0) == from_row, 1.0, 0.0
-        ).astype(BF)
-        r_t[:, cut] = jnp.where(
-            lax.broadcasted_iota(jnp.int32, (padded, tile), 0) == to_row, 1.0, 0.0
-        ).astype(BF)
-
-    todo = [(v, i) for v in (0, 1) for i in range(steps)]
-    pass_pair(*todo.pop(0))
+        to_row = to_row + jnp.where(to_row < 0, to_below, jnp.where(to_row >= own_m, to_above, 0))
+        mark(s_t, from_row, cut)
+        mark(r_t, to_row, cut)
+
     grid_swap.wait()
     grid_all = lambda: gridv[...].reshape(2 * rows_g, width)
     pg[...] = mm(wg_t[...], grid_all(), NT).astype(BF)
+    pass_pair(0, 0)
     edge_swap.wait()
     x_all = lambda: xv[...].reshape(edges, width)
-    for cut in cuts:
+    for t, cut in enumerate(cuts):
         pre_v[:, cut] = mm(pg[...], s_t[:, cut]) + mm(we_t[...], x_all()[cut], NT) + bcol
-        if todo:
-            pass_pair(*todo.pop(0))
-    for item in todo:
-        pass_pair(*item)
+        if t == 0:
+            for i in range(1, steps):
+                pass_pair(0, i)
+
+    near_rows, early = 2 * own_m, padded // 2
+    assert early <= near_rows
 
     def nodes(which):
         rows_in = win[which].reshape(window, width)
@@ -177,11 +193,34 @@
                 [rows_in, jnp.zeros((padded - window, width), BF)], axis=0)
         return rows_in
 
-    for i in range(steps):
+    def near_nodes(which):
+        return win[which, :2].reshape(near_rows, width)
+
+    def last_nodes(which):
+        return jnp.concatenate([
+            win[which, 2].reshape(own_m, width),
+            jnp.zeros((padded - window, width), BF)], axis=0)
+
+    for i in range(steps // 2):
+        pass_pair(1, i)
+    mesh_swap.wait()
+    shared(0, 1)
+    pm[:, :near_rows] = mm(near_nodes(0), wmv[...]).T.astype(BF)
+    for t, cut in enumerate(cuts):
+        pre_v[:, cut] += mm(pm[:, :early], r_t[:early, cut])
+        if t == tiles - 2:
+            pass_onward(0, 0)
+    for i in range(steps // 2, steps):
+        pass_pair(1, i)
+    for i in range(1, steps):
         pass_onward(0, i)
-    mesh_swap.wait()
-    shared(0)
-    pm[...] = mm(nodes(0), wmv[...]).T.astype(BF)
+    cot_swap.wait()
+    shared(1, 1)
+    pc[:, :near_rows] = mm(wov[...], near_nodes(1), NT).astype(BF)
+    for cut in cuts:
+        hid_v[:, cut] = mm(pc[:, :early], r_t[:early, cut])
+    shared(0, 2)
+    pm[:, near_rows:] = mm(last_nodes(0), wmv[...]).T.astype(BF)
     count = used[0]
     alive = [
         jnp.where(lax.broadcasted_iota(jnp.int32, (1, tile), 1) + t * tile < count, 1.0, 0.0)
@@ -189,18 +228,16 @@
     ]
     later = list(range(steps))
     for t, cut in enumerate(cuts):
-        pre = pre_v[:, cut] + mm(pm[...], r_t[:, cut])
+        pre = pre_v[:, cut] + mm(pm[:, early:], r_t[early:, cut])
         sig = jax.nn.sigmoid(pre)
         act_v[:, cut] = (pre * sig * alive[t]).astype(BF)
         pre_v[:, cut] = sig * (1.0 + pre * (1.0 - sig)) * alive[t]
-        if t >= 1 and later:
-            pass_onward(1, later.pop(0))
+        if t == 0:
+            pass_onward(1, 0)
+    for i in range(1, steps):
+        pass_onward(1, i)
     rsum[...] = mm(act_v[...], r_t[...], NT).astype(BF)
-
-    for i in later:
-        pass_onward(1, i)
-    cot_swap.wait()
-    shared(1)
+    shared(1, 2)
 
     far = lambda k: lax.rem(plane + k, high)
     near = lambda k: lax.rem(mine + k, 4)
@@ -237,17 +274,40 @@
 
     def step3(w, c):
         landed(2, w, c, in2.at[w, c, pl.ds(1, high - 1)])
-        for k in (1, 3, 2):
-            to(3, w, c, out1.at[w, c], out.at[w, c, mine], peer(k))
+        if w in SPLIT:
+            to(3, w, c, out1.at[w, c], in1.at[w, c, 0], along(second(c)))
+        else:
+            for k in (1, 3, 2):
+                to(3, w, c, out1.at[w, c], out.at[w, c, mine], peer(k))
         keep(w, c).start()
 
     def step4(w, c):
-        landed(3, w, c, in1.at[w, c, pl.ds(1, 3)])
+        if w in SPLIT:
+            landed(3, w, c, in1.at[w, c, 0])
+            to(4, w, c, out1.at[w, c], out.at[w, c, mine], along(first(c)))
+            to(4, w, c, in1.at[w, c, 0], out.at[w, c, flipped(second(c))], along(first(c)))
+            keep_landed(w, c).start()
+        else:
+            landed(3, w, c, in1.at[w, c, pl.ds(1, 3)])
+
+    def step5(w, c):
+        if w in SPLIT:
+            landed(4, w, c, in1.at[w, c, pl.ds(1, 2)])
+
+    first = lambda c: c % 2
+    second = lambda c: 1 - c % 2
+    shift = lambda bit: (1 - 2 * bits[bit]) * (1 + bit)
+    along = lambda bit: at(me + shift(bit))
+    flipped = lambda bit: mine + shift(bit)
+
+    def keep_landed(w, c):
+        return pltpu.make_async_copy(
+            in1.at[w, c, 0], out.at[w, c, flipped(second(c))], local.at[14])
 
     def keep(w, c):
         return pltpu.make_async_copy(out1.at[w, c], out.at[w, c, mine], local.at[15])
 
-    stages = ((step1, STAGE[0]), (step2, STAGE[1]), (step3, STAGE[2]), (step4, STAGE[3]))
+    stages = (step1, step2, step3, step4, step5)
 
     def bias_low(k):
         return remote(gb_own, gb_in.at[k], send.at[4], recv.at[4], peer(k))
@@ -255,13 +315,14 @@
     def bias_high(k):
         return remote(gb_sum, gb_all.at[k], send.at[5], recv.at[5], distant(k))
 
+    parts = range(rx.shape[1])
     rx_on = [
-        remote(rx.at[2 * odd, i], rims.at[0, i], send.at[9 + i], recv.at[9 + i], at(backward))
-        for i in (0, 1)
+        remote(rx.at[2, i], rims.at[0, i], send.at[9 + i], recv.at[9 + i], at(backward))
+        for i in parts
     ]
     rx_pair = [
-        remote(rxs.at[i], rims.at[1, i], send.at[11 + i], recv.at[11 + i], at(pair))
-        for i in (0, 1)
+        remote(rxs.at[i], rims.at[1, i], send.at[3 + 10 + i], recv.at[3 + 10 + i], at(pair))
+        for i in parts
     ]
     grid_copy = remote(gg_v.at[1 - half], gg_in, send.at[6], recv.at[6], partner)
     edge_copy = remote(ge_v.at[1 - half], ge_in, send.at[7], recv.at[7], partner)
@@ -275,17 +336,17 @@
     grid_sum = (grid_copy, gg_v, gg_in, grid_out, 11)
     edge_sum = (edge_copy, ge_v, ge_in, edge_out, 12)
     mesh_sum = (mesh_copy, gm_v, gm_in, mesh_out, 13)
-    bias_done = pltpu.make_async_copy(gb_out, bias_out, local.at[14])
+    bias_done = pltpu.make_async_copy(gb_out, bias_out, local.at[16])
 
     def rx_step1(i):
         rx_on[i].wait()
-        rxs[i] = (rx[2 - 2 * odd, i].astype(F32) + rims[0, i].astype(F32)).astype(BF)
+        rxs[i] = (rx[1, i].astype(F32) + rims[0, i].astype(F32)).astype(BF)
         rx_pair[i].start()
 
     def rx_step2():
         for copy in rx_pair:
             copy.wait()
-        total = (rx[1].astype(F32) + rims[1].astype(F32)).astype(BF).reshape(own_m, hidden)
+        total = (rx[0].astype(F32) + rims[1].astype(F32)).astype(BF).reshape(own_m, hidden)
         gm_v[...] = mm(total, wmv[...], NT).astype(BF).reshape(gm_v.shape)
         mesh_copy.start()
 
@@ -303,15 +364,14 @@
         gb_out[...] = jnp.sum(gb_all[...], axis=0)
         bias_done.start()
 
-    keepsake = {}
-
     def make_wo():
         offer(WO, mm(rsum[...], nodes(1)))
 
     def make_hidden():
-        pm[...] = mm(wov[...], nodes(1), NT).astype(BF)
+        pc[:, near_rows:] = mm(wov[...], last_nodes(1), NT).astype(BF)
         for cut in cuts:
-            pc_v[:, cut] = (mm(pm[...], r_t[:, cut]) * pre_v[:, cut]).astype(BF)
+            hidden_cot = hid_v[:, cut] + mm(pc[:, early:], r_t[early:, cut])
+            pc_v[:, cut] = (hidden_cot * pre_v[:, cut]).astype(BF)
 
     def make_we():
         offer(WE, mm(pc_v[...], x_all()))
@@ -329,12 +389,17 @@
         offer(WM, mm(sr.astype(BF), nodes(0)))
         rx[...] = sr.T[:window].astype(BF).reshape(rx.shape)
 
+    split = rows_g // 128 * 128 + 128
+
+    def make_sg():
+        sg[:, :split] = mm(pc_v[...], s_t[:split], NT).astype(BF)
+
     def make_wg():
-        keepsake["sg"] = mm(pc_v[...], s_t[...], NT).astype(BF)
-        offer(WG, mm(keepsake["sg"], grid_all()))
+        sg[:, split:] = mm(pc_v[...], s_t[split:], NT).astype(BF)
+        offer(WG, mm(sg[...], grid_all()))
 
     def make_grid():
-        gg_v[...] = mm(keepsake["sg"], wg_t[...], TN).astype(BF).reshape(gg_v.shape)
+        gg_v[...] = mm(sg[...], wg_t[...], TN).astype(BF).reshape(gg_v.shape)
         grid_copy.start()
 
     def make_edge():
@@ -342,30 +407,30 @@
         edge_copy.start()
 
     PLAN = (
-        (8.2, "rx0a", lambda now: rx_on[0].start()),
-        (8.2, "rx0b", lambda now: rx_on[1].start()),
-        (12.5, "rx1a", lambda now: rx_step1(0)),
-        (14.0, "rx1b", lambda now: rx_step1(1)),
+        (11.1, "rx0a", lambda now: rx_on[0].start()),
+        (15.6, "rx1a", lambda now: rx_step1(0)),
+        (12.5, "rx0b", lambda now: rx_on[1].start()),
+        (16.6, "rx1b", lambda now: rx_step1(1)),
+        (13.6, "rx0c", lambda now: rx_on[2].start()),
+        (17.8, "rx1c", lambda now: rx_step1(2)),
+        (15.0, "rx0d", lambda now: rx_on[3].start()),
+        (19.0, "rx1d", lambda now: rx_step1(3)),
         (15.0, "bias1", lambda now: bias_step1()),
-        (12.0, "set_grid", lambda now: settle(*grid_sum)),
-        (13.0, "set_edge", lambda now: settle(*edge_sum)),
-        (18.0, "rx2", lambda now: rx_step2()),
-        (20.5, "set_mesh", lambda now: settle(*mesh_sum)),
-        (19.0, "bias2", lambda now: bias_step2()),
+        (12.2, "set_grid", lambda now: settle(*grid_sum)),
+        (12.3, "set_edge", lambda now: settle(*edge_sum)),
+        (24.5, "rx2", lambda now: rx_step2()),
+        (26.5, "set_mesh", lambda now: settle(*mesh_sum)),
+        (21.5, "bias2", lambda now: bias_step2()),
     )
     events = []
 
     def plan(time, name, fn):
         events.append((time, len(events), name, fn))
 
-    def chain(time, w, c, stage):
-        fn, lasts = stages[stage]
-
-        def run(now):
-            fn(w, c)
-            if stage < len(stages) - 1:
-                chain(max(now, time + lasts), w, c, stage + 1)
-        plan(time + lasts, f"s{stage + 1}_{w}{c}", run)
+    def chain(time, w, c):
+        for fn, lasts in zip(stages, STAGE):
+            time = time + lasts
+            plan(time, f"{fn.__name__}_{w}{c}", lambda now, fn=fn: fn(w, c))
 
     def due(now):
         while events and min(events)[0] <= now:
@@ -374,15 +439,17 @@
             event[3](max(now, event[0]) if now < 1e6 else event[0])
 
     def offered(w):
-        return lambda now: [chain(now, w, c, 0) for c in range(cuts_w)]
+        return lambda now: [
+            chain(max(now + 2.2, 2.65) + 1.4 * (c + 1) + 0.8 * w, w, c) for c in range(cuts_w)]
 
     now = 0.0
     for name, fn, lasts, after in (
-        ("gwo", make_wo, 0.4, offered(WO)),
-        ("hid", make_hidden, 1.8, None),
+        ("gwo", make_wo, 0.45, offered(WO)),
+        ("hid", make_hidden, 1.2, None),
         ("gwe", make_we, 0.8, offered(WE)),
-        ("sr", make_wm, 1.7, offered(WM)),
-        ("sg", make_wg, 2.7, offered(WG)),
+        ("sr", make_wm, 1.95, offered(WM)),
+        ("sg", make_sg, 1.3, None),
+        ("gwg", make_wg, 1.3, offered(WG)),
         ("bias", make_bias, 0.2, None),
         ("gradgrid", make_grid, 0.5, None),
         ("gradedge", make_edge, 0.8, None),
@@ -398,8 +465,8 @@
     for copy, own, _, to, i in (grid_sum, edge_sum, mesh_sum):
         pltpu.make_async_copy(own.at[half], to, local.at[i]).wait()
     bias_done.wait()
-    kept = out1.at[...]
-    pltpu.make_async_copy(kept, kept, local.at[15]).wait()
+    for kept, i in ((out1, 15),):
+        pltpu.make_async_copy(kept, kept, local.at[i]).wait()
     for v in (0, 1):
         ref = win.at[v, pl.ds(0, 2)]
         remote(ref, ref, wins.at[v], pr.at[v], partner).wait_send()
@@ -408,18 +475,44 @@
 def final_kernel(
     grid_sum, edge_sum, mesh_sum, out, bias_sum,
     grad_grid, grad_edge, grad_mesh, gwg, gwm, gwe, gbias, gwo,
+    gv, ev, mv, outv, bv, wide, tall, flat, came, went,
 ):
-    grad_grid[...] = grid_sum[...]
-    grad_edge[...] = edge_sum[...]
-    grad_mesh[...] = mesh_sum[...]
-    cuts = range(out.shape[1])
-    full = lambda w: jnp.concatenate(
-        [out[w, c].astype(F32).reshape(gwo.shape[0], -1) for c in cuts], axis=1)
-    gwg[...] = full(WG).T
-    gwe[...] = full(WE).T
-    gwm[...] = full(WM).T
-    gwo[...] = full(WO)
-    gbias[...] = bias_sum[...][0]
+    rows = ev.shape[0] // 2
+    halves = [pl.ds(i * rows, rows) for i in (0, 1)]
+    passing = [
+        (edge_sum.at[halves[0]], ev.at[halves[0]], grad_edge.at[halves[0]]),
+        (edge_sum.at[halves[1]], ev.at[halves[1]], grad_edge.at[halves[1]]),
+        (grid_sum, gv, grad_grid), (mesh_sum, mv, grad_mesh),
+    ]
+    copy = pltpu.make_async_copy
+    into = [copy(out.at[w], outv.at[w], came.at[w]) for w in range(4)]
+    into.append(copy(bias_sum, bv, came.at[8]))
+    take = [copy(src, mid, came.at[4 + i]) for i, (src, mid, _) in enumerate(passing)]
+    give = [copy(mid, dst, went.at[4 + i]) for i, (_, mid, dst) in enumerate(passing)]
+    done = [
+        copy(wide, gwo, went.at[WO]), copy(tall.at[0], gwe, went.at[WE]),
+        copy(tall.at[1], gwm, went.at[WM]), copy(tall.at[2], gwg, went.at[WG]),
+    ]
+    for read in (into[0], take[0], into[1], take[1], into[2], take[2], into[3], take[3], into[4]):
+        read.start()
+    for w in range(4):
+        into[w].wait()
+        value = jnp.concatenate([
+            outv[w, c].astype(F32).reshape(wide.shape[0], -1) for c in range(outv.shape[1])
+        ], axis=1)
+        if w == WO:
+            wide[...] = value
+        else:
+            tall[w - 1] = value.T
+        done[w].start()
+        take[w].wait()
+        give[w].start()
+    into[4].wait()
+    flat[...] = bv[...][0]
+    last = copy(flat, gbias, went.at[8])
+    last.start()
+    for write in done + give + [last]:
+        write.wait()
 
 
 def body(
@@ -453,6 +546,7 @@
     rows_c = hidden // n
     cuts_w, steps = 2, 2
     piece = (rows_c, width // cuts_w)
+    rim = (4, own_m // 4, hidden)
     edge_sum, grid_sum, mesh_sum, out, bias_sum = pl.pallas_call(
         functools.partial(mega_kernel, tile),
         out_shape=(
@@ -469,22 +563,22 @@
             vm((edges,), jnp.int32), vm((edges,), jnp.int32),
             vm((hidden, width), BF), vm((hidden, width), BF),
             vm((2 * rows_g, edges), BF), vm((padded, edges), BF),
-            vm((hidden, 2 * rows_g), BF), vm((hidden, padded), BF),
-            vm((hidden, edges), F32), vm((hidden, edges), BF), vm((hidden, edges), BF),
+            vm((hidden, 2 * rows_g), BF), vm((hidden, padded), BF), vm((hidden, padded), BF),
+            vm((hidden, edges), F32), vm((hidden, edges), F32), vm((hidden, edges), BF), vm((hidden, edges), BF),
+            vm((hidden, 2 * rows_g), BF),
             vm((hidden, padded), BF),
             vm((2, rows_e, width), BF), vm((rows_e, width), BF),
             vm((2, rows_g, width), BF), vm((rows_g, width), BF),
-            vm((3, 2, rows_m, hidden), BF), vm((2, 2, rows_m, hidden), BF),
-            vm((2, rows_m, hidden), BF),
+            vm((3,) + rim, BF), vm((2,) + rim, BF), vm(rim, BF),
             vm((2, rows_m, width), BF), vm((rows_m, width), BF),
             vm((4, cuts_w, 4, high) + piece, BF), vm((4, cuts_w, 4, high) + piece, BF),
             vm((4, cuts_w, high) + piece, BF), vm((4, cuts_w, high) + piece, BF),
             vm((4, cuts_w) + piece, BF), vm((4, cuts_w, high) + piece, BF),
             vm((8, hidden), F32), vm((4, 8, hidden), F32), vm((8, hidden), F32),
             vm((high, 8, hidden), F32), vm((8, hidden), F32),
-            dma((16,)), dma((13,)), dma((13,)),
+            dma((17,)), dma((17,)), dma((17,)),
             dma((2,)), dma((2, steps)), dma((2, steps)), dma((2,)), dma((2,)),
-            dma((4, cuts_w)), dma((4, 4, cuts_w)),
+            dma((4, cuts_w)), dma((5, 4, cuts_w)),
         ],
         compiler_params=pltpu.CompilerParams(
             collective_id=0, has_side_effects=True, vmem_limit_bytes=60 * 2**20),
@@ -493,27 +587,21 @@
         w_grid, w_edge, w_mesh, w_out, bias, senders, receivers,
     )
 
-    rows_of = lambda rows: pl.BlockSpec((rows // 2, width), lambda t: (t, 0))
-    turned_spec = pl.BlockSpec((width, hidden // 2), lambda t: (0, t))
     return pl.pallas_call(
         final_kernel,
-        grid=(2,),
-        in_specs=[
-            rows_of(rows_g), rows_of(rows_e), rows_of(rows_m),
-            pl.BlockSpec((4, cuts_w, n // 2) + piece, lambda t: (0, 0, t, 0, 0)),
-            pl.BlockSpec((8, hidden), lambda t: (0, 0)),
-        ],
-        out_specs=(
-            rows_of(rows_g), rows_of(rows_e), rows_of(rows_m),
-            turned_spec, turned_spec, turned_spec,
-            pl.BlockSpec((hidden,), lambda t: (0,)), rows_of(hidden),
-        ),
+        in_specs=[ANY] * 5,
+        out_specs=(ANY,) * 8,
         out_shape=(
             sds((rows_g, width), BF), sds((rows_e, width), BF), sds((rows_m, width), BF),
             sds((width, hidden), F32), sds((width, hidden), F32), sds((width, hidden), F32),
             sds((hidden,), F32), sds((hidden, width), F32),
         ),
-        compiler_params=pltpu.CompilerParams(dimension_semantics=("arbitrary",)),
+        scratch_shapes=[
+            vm((rows_g, width), BF), vm((rows_e, width), BF), vm((rows_m, width), BF),
+            vm((4, cuts_w, n) + piece, BF), vm((8, hidden), F32),
+            vm((hidden, width), F32), vm((3, width, hidden), F32), vm((hidden,), F32),
+            dma((9,)), dma((9,)),
+        ],
     )(grid_sum, edge_sum, mesh_sum, out.reshape((4, cuts_w, n) + piece), bias_sum)
 
 

time: 62.9 us -> 58.5 us (0.930)
  Pallas kernels: 61.2 us -> 56.9 us
    pallas_call x1, Pallas kernels: 57.8 us -> 53.8 us  [body(): pl.pallas_call(functools.partial(mega_kernel, tile), out_shape=(sds((rows...]
where the time goes in v3:
time: 58.5 us; the launch traced here: 58.3 us
  Pallas kernels  56.9 us (97%)
  between operations  1.45 us (2%)
    pallas_call x1, Pallas kernels, body(): pl.pallas_call(functools.partial(mega_kernel, tile), out_shape=(sds((rows...  53.8 us
    pallas_call x1, Pallas kernels, body(): pl.pallas_call(final_kernel, in_specs=[ANY] * 5, out_specs=(ANY,) * 8, ou...  3.08 us

profile of v3, /device:TPU:0, one launch (start us, length us, event | category | flops | bytes accessed | tf_op | source)
XLA Modules:
  0.0 58.3 jit_solution(15132025139813146108)
XLA Ops:
  1.3 53.8 %shard_map.179 = (bf16[1152,512]{1,0:T(8,128)(2,1)}, bf16[576,512]{1,0:T(8,128)(2,1)}, bf16[160,512]{1,0:T(8,128)(2,1)}, bf16[4,2,4,4,16,256]{5,4,3,2,1,0:T(8,128)(2,1)}, f32[8,256]{1,0:T(8,128)}) custom-call(s32[1]{0:T(128)S(6)} %copy.20.used, bf16[576,512]{1,0:T(8,128)(2,1)} %grid.1, bf16[1152,512]{1,0:T(8,128)(2,1)} %edge.1, bf16[160,512]{1,0:T(8,128)(2,1)} %mesh.1, ...), custom_call_target="tpu_custom_call" | custom-call | tf_op jit(solution)/shard_map/pallas_call | solution.py:550
  55.1 3.1 %shard_map.180 = (bf16[576,512]{1,0:T(8,128)(2,1)}, bf16[1152,512]{1,0:T(8,128)(2,1)}, bf16[160,512]{1,0:T(8,128)(2,1)}, f32[512,256]{1,0:T(8,128)}, f32[512,256...) custom-call(bf16[576,512]{1,0:T(8,128)(2,1)} %get-tuple-element.13.grid_sum, ...), custom_call_target="tpu_custom_call" | custom-call | tf_op jit(solution)/shard_map/pallas_call | solution.py:590

commit v4 on v3

--- a/solution.py
+++ b/solution.py
@@ -210,8 +210,8 @@
         pre_v[:, cut] += mm(pm[:, :early], r_t[:early, cut])
         if t == tiles - 2:
             pass_onward(0, 0)
-    for i in range(steps // 2, steps):
-        pass_pair(1, i)
+            for i in range(steps // 2, steps):
+                pass_pair(1, i)
     for i in range(1, steps):
         pass_onward(0, i)
     cot_swap.wait()
@@ -429,7 +429,7 @@
 
     def chain(time, w, c):
         for fn, lasts in zip(stages, STAGE):
-            time = time + lasts
+            time = time + lasts + (1.5 if fn is step4 and w not in SPLIT else 0.0)
             plan(time, f"{fn.__name__}_{w}{c}", lambda now, fn=fn: fn(w, c))
 
     def due(now):
@@ -465,8 +465,7 @@
     for copy, own, _, to, i in (grid_sum, edge_sum, mesh_sum):
         pltpu.make_async_copy(own.at[half], to, local.at[i]).wait()
     bias_done.wait()
-    for kept, i in ((out1, 15),):
-        pltpu.make_async_copy(kept, kept, local.at[i]).wait()
+    pltpu.make_async_copy(out1, out1, local.at[15]).wait()
     for v in (0, 1):
         ref = win.at[v, pl.ds(0, 2)]
         remote(ref, ref, wins.at[v], pr.at[v], partner).wait_send()

time: 58.5 us -> 57.7 us (0.986)
  Pallas kernels: 56.9 us -> 56.1 us
    pallas_call x1, Pallas kernels: 53.8 us -> 53 us  [body(): pl.pallas_call(functools.partial(mega_kernel, tile), out_shape=(sds((rows...]
where the time goes in v4:
time: 57.7 us; the launch traced here: 57.5 us
  Pallas kernels  56.1 us (97%)
  between operations  1.45 us (3%)
    pallas_call x1, Pallas kernels, body(): pl.pallas_call(functools.partial(mega_kernel, tile), out_shape=(sds((rows...  53 us
    pallas_call x1, Pallas kernels, body(): pl.pallas_call(final_kernel, in_specs=[ANY] * 5, out_specs=(ANY,) * 8, ou...  3.08 us

profile of v4, /device:TPU:0, one launch (start us, length us, event | category | flops | bytes accessed | tf_op | source)
XLA Modules:
  0.0 57.5 jit_solution(8713091533036491145)
XLA Ops:
  1.3 53.0 %shard_map.179 = (bf16[1152,512]{1,0:T(8,128)(2,1)}, bf16[576,512]{1,0:T(8,128)(2,1)}, bf16[160,512]{1,0:T(8,128)(2,1)}, bf16[4,2,4,4,16,256]{5,4,3,2,1,0:T(8,128)(2,1)}, f32[8,256]{1,0:T(8,128)}) custom-call(s32[1]{0:T(128)S(6)} %copy.20.used, bf16[576,512]{1,0:T(8,128)(2,1)} %grid.1, bf16[1152,512]{1,0:T(8,128)(2,1)} %edge.1, bf16[160,512]{1,0:T(8,128)(2,1)} %mesh.1, ...), custom_call_target="tpu_custom_call" | custom-call | tf_op jit(solution)/shard_map/pallas_call | solution.py:549
  54.3 3.1 %shard_map.180 = (bf16[576,512]{1,0:T(8,128)(2,1)}, bf16[1152,512]{1,0:T(8,128)(2,1)}, bf16[160,512]{1,0:T(8,128)(2,1)}, f32[512,256]{1,0:T(8,128)}, f32[512,256...) custom-call(bf16[576,512]{1,0:T(8,128)(2,1)} %get-tuple-element.13.grid_sum, ...), custom_call_target="tpu_custom_call" | custom-call | tf_op jit(solution)/shard_map/pallas_call | solution.py:589

commit v5 on v4

--- a/solution.py
+++ b/solution.py
@@ -239,8 +239,10 @@
     rsum[...] = mm(act_v[...], r_t[...], NT).astype(BF)
     shared(1, 2)
 
-    far = lambda k: lax.rem(plane + k, high)
-    near = lambda k: lax.rem(mine + k, 4)
+    sign = 1 - 2 * (plane // (high // 2))
+    far = lambda k: lax.rem(plane + sign * k + high, high)
+    turn = lambda bit, k: 1 - bits[bit] if (k >> bit) & 1 else bits[bit]
+    near = lambda k: turn(0, k) + 2 * turn(1, k)
     peer = lambda k: at(plane * 4 + near(k))
     distant = lambda k: at(far(k) * 4 + mine)
 
@@ -254,7 +256,7 @@
         part = width // cuts_w
         for c in range(cuts_w):
             gall[w, c] = value[:, c * part:(c + 1) * part].reshape(gall.shape[2:]).astype(BF)
-            for k in (1, 3, 2):
+            for k in (3, 1, 2):
                 to(0, w, c, gall.at[w, c, near(k)], in1.at[w, c, k], peer(k))
 
     def step1(w, c):
@@ -263,13 +265,15 @@
         for k in range(1, 4):
             total = total + in1[w, c, k].astype(F32)
         sum1[w, c] = total.astype(BF)
-        each(1, high, lambda k: to(1, w, c, sum1.at[w, c, far(k)], in2.at[w, c, k], distant(k)))
+        each(1, high, lambda k: to(
+            1, w, c, sum1.at[w, c, far(high - k)], in2.at[w, c, plane], distant(high - k)))
 
     def step2(w, c):
         landed(1, w, c, in2.at[w, c, pl.ds(1, high - 1)])
-        in2[w, c, 0] = sum1[w, c, plane]
+        in2[w, c, plane] = sum1[w, c, plane]
         sum2[w, c] = jnp.sum(in2[w, c].astype(F32), axis=0).astype(BF)
-        each(1, high, lambda k: to(2, w, c, sum2.at[w, c], out1.at[w, c, plane], distant(k)))
+        each(1, high, lambda k: to(
+            2, w, c, sum2.at[w, c], out1.at[w, c, plane], distant(high - k)))
         out1[w, c, plane] = sum2[w, c]
 
     def step3(w, c):
@@ -277,7 +281,7 @@
         if w in SPLIT:
             to(3, w, c, out1.at[w, c], in1.at[w, c, 0], along(second(c)))
         else:
-            for k in (1, 3, 2):
+            for k in (3, 1, 2):
                 to(3, w, c, out1.at[w, c], out.at[w, c, mine], peer(k))
         keep(w, c).start()
 
@@ -313,7 +317,7 @@
         return remote(gb_own, gb_in.at[k], send.at[4], recv.at[4], peer(k))
 
     def bias_high(k):
-        return remote(gb_sum, gb_all.at[k], send.at[5], recv.at[5], distant(k))
+        return remote(gb_sum, gb_all.at[plane], send.at[5], recv.at[5], distant(k))
 
     parts = range(rx.shape[1])
     rx_on = [
@@ -360,7 +364,7 @@
     def bias_step2():
         ref = gb_all.at[pl.ds(1, high - 1)]
         remote(ref, ref, send.at[5], recv.at[5], partner).wait()
-        gb_all[0] = gb_sum[...]
+        gb_all[plane] = gb_sum[...]
         gb_out[...] = jnp.sum(gb_all[...], axis=0)
         bias_done.start()
 

time: 57.7 us -> 57.6 us (level)
  no operation moved by 1% of the time
where the time goes in v5:
time: 57.6 us; the launch traced here: 57.4 us
  Pallas kernels  55.9 us (97%)
  between operations  1.45 us (3%)
    pallas_call x1, Pallas kernels, body(): pl.pallas_call(functools.partial(mega_kernel, tile), out_shape=(sds((rows...  52.9 us
    pallas_call x1, Pallas kernels, body(): pl.pallas_call(final_kernel, in_specs=[ANY] * 5, out_specs=(ANY,) * 8, ou...  3.08 us

profile of v5, /device:TPU:0, one launch (start us, length us, event | category | flops | bytes accessed | tf_op | source)
XLA Modules:
  0.0 57.4 jit_solution(6542653475412927524)
XLA Ops:
  1.3 52.9 %shard_map.179 = (bf16[1152,512]{1,0:T(8,128)(2,1)}, bf16[576,512]{1,0:T(8,128)(2,1)}, bf16[160,512]{1,0:T(8,128)(2,1)}, bf16[4,2,4,4,16,256]{5,4,3,2,1,0:T(8,128)(2,1)}, f32[8,256]{1,0:T(8,128)}) custom-call(s32[1]{0:T(128)S(6)} %copy.20.used, bf16[576,512]{1,0:T(8,128)(2,1)} %grid.1, bf16[1152,512]{1,0:T(8,128)(2,1)} %edge.1, bf16[160,512]{1,0:T(8,128)(2,1)} %mesh.1, ...), custom_call_target="tpu_custom_call" | custom-call | tf_op jit(solution)/shard_map/pallas_call | solution.py:553
  54.1 3.1 %shard_map.180 = (bf16[576,512]{1,0:T(8,128)(2,1)}, bf16[1152,512]{1,0:T(8,128)(2,1)}, bf16[160,512]{1,0:T(8,128)(2,1)}, f32[512,256]{1,0:T(8,128)}, f32[512,256...) custom-call(bf16[576,512]{1,0:T(8,128)(2,1)} %get-tuple-element.13.grid_sum, ...), custom_call_target="tpu_custom_call" | custom-call | tf_op jit(solution)/shard_map/pallas_call | solution.py:593
